TPU v7x, 256 devices: a whole 4x4x8 slice. The times are simulated.
256 devices in a mesh: rep: 1, dp: 256 (over x, y, z, core).
Axes of the slice: x: 4, y: 4, z: 8, core: 2. Of those that a mesh axis runs over, the one named last changes fastest.
Arguments:
- x: bfloat16 [256, 1024, 1024], P(('rep', 'dp'))
- dy: bfloat16 [256, 1024, 1024], P(('rep', 'dp'))
- w_gate: bfloat16 [2, 1024, 2560], replicated
- w_up: bfloat16 [2, 1024, 2560], replicated
- w_down: bfloat16 [2, 2560, 1024], replicated
- m_w_gate: float32 [2, 1024, 2560], P(None, 'dp')
- m_w_up: float32 [2, 1024, 2560], P(None, 'dp')
- m_w_down: float32 [2, 2560, 1024], P(None, 'dp')
- v_w_gate: float32 [2, 1024, 2560], P(None, 'dp')
- v_w_up: float32 [2, 1024, 2560], P(None, 'dp')
- v_w_down: float32 [2, 2560, 1024], P(None, 'dp')
Outputs:
- output 1: bfloat16 [2, 1024, 2560], P('rep')
- output 2: bfloat16 [2, 1024, 2560], P('rep')
- output 3: bfloat16 [2, 2560, 1024], P('rep')
- output 4: float32 [2, 1024, 2560], P('rep', 'dp')
- output 5: float32 [2, 1024, 2560], P('rep', 'dp')
- output 6: float32 [2, 2560, 1024], P('rep', 'dp')
- output 7: float32 [2, 1024, 2560], P('rep', 'dp')
- output 8: float32 [2, 1024, 2560], P('rep', 'dp')
- output 9: float32 [2, 2560, 1024], P('rep', 'dp')
All inputs are finite; a program needn't handle non-finite values.
Results may differ from a plain program's by a relative error of at most 0.022.
Values are sent between devices in bfloat16 or wider.
A program may use at most 768 MiB of HBM per device.

v0:
```python
import functools

import jax
import jax.numpy as jnp
from jax import lax
from jax.experimental import pallas as pl
from jax.experimental.pallas import tpu as pltpu
from jax.sharding import PartitionSpec as P

NAMES = ("w_gate", "w_up", "w_down")
MESH = pl.DeviceIdType.MESH
F32, BF16 = jnp.float32, jnp.bfloat16
SIZES = {"x": 4, "y": 4, "z": 8}
VMEM_LIMIT = 64 * 1024 * 1024 - 64 * 1024

TICKS = {
    "first": ["0h"],
    "wide1": ["1h", "1s", "2h020100", "12110210222120"],
    "back": ["", "01001202", "111022", "", "122120010002", "111022", "1202210020", "0111102202001221200111021022202112000103221112101303"],
    "units": ["1321202223", "", "23", "", "", "", "", "", "", ""],
    "last": ["3h"],
    "wide0": ["4h", "4s", "5h323130", "42413240525150"],
    "tail": ["3130423241405242515032313052414042513230504031415251304231324140505251324230503133524142404351334352505353"],
}
GATHER_ORDER = "020100121110222120023231301242412240013202525150004211125210220121002032104211003120300110215241110240203051501200310122321011214240413050520220511201110122001132213140500010414210522102302112203151222032414042525002021231302212323140514230223252414050425241515051"


RING, DIRECT = "ring", "direct"
COLOURS = (
    (("x", RING), ("y", RING), ("z", DIRECT)),
    (("y", RING), ("x", RING), ("z", DIRECT)),
    (("z", RING), ("x", DIRECT), ("y", DIRECT)),
)
WIDE, TALL = "wide", "tall"
PART = {WIDE: ((0, 384), (384, 384), (768, 512)), TALL: ((0, 16), (16, 16), (32, 8))}
HALF = {WIDE: 1280, TALL: 512}
ROWS = {WIDE: 8, TALL: 40}
ORDER = ((TALL, 1), (WIDE, 1), (WIDE, 3), (TALL, 0), (WIDE, 0), (WIDE, 2))


class Me:
    def __init__(self):
        index = lax.axis_index("dp")
        Me.zero = index * 0
        self.core = lax.rem(index, 2)
        chip = index // 2
        self.at = {
            "z": lax.rem(chip, SIZES["z"]),
            "y": lax.rem(chip // SIZES["z"], SIZES["y"]),
            "x": chip // (SIZES["z"] * SIZES["y"]),
        }
        self.sign = 1 - 2 * self.core

    def off(self, d, by):
        return lax.rem(self.at[d] + by + SIZES[d], SIZES[d])

    def device(self, core=None, **at):
        at = {**self.at, **at}
        core = self.core if core is None else core
        return (0, ((at["x"] * SIZES["y"] + at["y"]) * SIZES["z"] + at["z"]) * 2 + core)

    def barrier(self):
        sem = pltpu.get_barrier_semaphore()

        def signal(peer):
            pl.semaphore_signal(sem, inc=1, device_id=peer, device_id_type=MESH)

        for d, n in SIZES.items():
            each(n - 1, lambda i, d=d: signal(self.device(**{d: self.off(d, i + 1)})))
        signal(self.device(core=1 - self.core))
        signal(self.device(core=1 - self.core, z=self.pair()))
        pl.semaphore_wait(sem, sum(SIZES.values()) - 1)

    def pair(self):
        return self.at["z"] + 1 - 2 * lax.rem(self.at["z"], 2)


def dims(kind, free):
    return tuple(SIZES[d] // (2 if kind == TALL and d == "z" else 1) for d in free)


def view(ref, kind, free, fixed, colour=None, base=0, own=False):
    index = [(fixed[d] // 2 if kind == TALL and d == "z" else fixed[d]) if d in fixed else slice(None) for d in free]
    if own and not (kind == TALL and "z" in free and "z" in fixed):
        return ref.at[(*index, slice(None), slice(None))]
    if kind == WIDE:
        first, size = (0, HALF[WIDE]) if colour is None else PART[WIDE][colour]
        rows, columns = slice(None), pl.ds(_at(base, first), size)
    else:
        rows = slice(None) if own or colour is None else pl.ds(*PART[TALL][colour])
        if "z" in free and "z" in fixed:
            columns = pl.ds(pl.multiple_of(base + lax.rem(fixed["z"], 2) * 256, 256), 256)
        else:
            columns = pl.ds(_at(base, 0), HALF[TALL])
    return ref.at[(*index, rows, columns)]


def _at(base, first):
    return first if isinstance(base, int) and base == 0 else pl.multiple_of(base + first, 128)


def block(kind, colour, free):
    first, size = PART[kind][colour]
    tail = (8, size) if kind == WIDE else (size, HALF[TALL] if "z" in free else HALF[TALL] // 2)
    return dims(kind, free) + tail


def lengths(n):
    return n // 2, (n - 1) // 2


def reduce_buffers(kind):
    shapes = {}
    for c, phases in enumerate(COLOURS):
        free = ["x", "y", "z"]
        for p, (d, how) in enumerate(phases):
            free.remove(d)
            shape = block(kind, c, tuple(free))
            count = SIZES[d] - 1
            shapes[c, p] = (count, *shape)
    return shapes


class Copies:
    def __init__(self, send, recv):
        self.send, self.recv, self.all, self.used, self.left = send, recv, {}, 0, set()

    def start(self, key, make):
        self.start_all(key, 1, lambda i: make())

    def start_all(self, key, count, make):
        first = self.used
        self.used += count

        def copy(i):
            src, dst, to = make(i)
            return pltpu.make_async_remote_copy(
                src_ref=src, dst_ref=dst, send_sem=self.send.at[first + i], recv_sem=self.recv.at[first + i], device_id=to, device_id_type=MESH
            )

        self.all[key] = count, copy
        each(count, lambda i: copy(i).start())

    def arrived(self, key):
        count, copy = self.all[key]
        each(count, lambda i: copy(i).wait_recv())

    def sent(self, mine=lambda key: True):
        for key, (count, copy) in self.all.items():
            if key not in self.left and mine(key):
                self.left.add(key)
                each(count, lambda i, copy=copy: copy(i).wait_send())


def each(count, do):
    if count == 1:
        do(0)
    else:

        loop(count)(do)


def loop(count):
    def run(body):
        def step(carry, _):
            body(carry[0])
            return (carry[0] + 1, None), None

        lax.scan(step, (Me.zero, None), None, length=count)

    return run


def total(parts):
    return functools.reduce(jnp.add, [p[...].astype(F32) for p in parts])


def reduce_colour(me, copies, key, kind, colour, grads, received, last):
    free, fixed = ("x", "y", "z"), {}
    parts = [lambda at, r=r: view(r(), kind, ("x", "y", "z"), at, colour) for r in grads]
    out = parts[0]

    def add(at, more):
        rest = [d for d in free if d not in at]
        if len(rest) >= 2:
            first = rest[0]

            @loop(SIZES[first])
            def _(i):
                now = {**at, first: i}
                out(now)[...] = total([p(now) for p in parts + more]).astype(BF16)
        else:
            out(at)[...] = total([p(at) for p in parts + more]).astype(BF16)

    for phase, (d, how) in enumerate(COLOURS[colour]):
        n, buffer = SIZES[d], functools.partial(received, colour, phase)
        left = tuple(e for e in ("x", "y", "z") if e not in fixed and e != d)

        def slot(i, buffer=buffer, left=left):
            return lambda at: view(buffer().at[i], kind, left, {e: v for e, v in at.items() if e in left}, colour, own=True)

        if how == RING:
            long, short = lengths(n)
            ways = ((1, long, 0, "l"), (-1, short, long, "s"))
            for s in range(long):
                for sign, length, base, name in ways:
                    if s >= length:
                        continue

                    def make(d=d, fixed=fixed, buffer=buffer, sign=sign, by=length - s, place=base + s):
                        at = {**fixed, d: me.off(d, me.sign * (sign * by))}
                        return out(at), buffer().at[place], me.device(**{d: me.off(d, me.sign * sign)})

                    if s:
                        copies.arrived((key, colour, phase, name, s - 1))
                    add({**fixed, d: me.off(d, me.sign * (sign * (length - s)))}, [slot(base + s - 1)] if s else [])
                    copies.start((key, colour, phase, name, s), make)
                yield
            for sign, length, base, name in ways:
                if length:
                    copies.arrived((key, colour, phase, name, length - 1))
            parts = parts + [slot(base + length - 1) for sign, length, base, name in ways if length]
        else:

            def make(i, d=d, fixed=fixed, buffer=buffer, add=add, out=out):
                to = me.off(d, i + 1)
                return out({**fixed, d: to}), buffer().at[i], me.device(**{d: to})

            each(n - 1, lambda i: add({**fixed, d: me.off(d, i + 1)}, []))
            copies.start_all((key, colour, phase), n - 1, make)
            yield
            copies.arrived((key, colour, phase))
            parts = parts + [slot(i) for i in range(n - 1)]
        fixed = {**fixed, d: me.at[d]}
    last(colour, total([p(fixed) for p in parts]).astype(BF16).astype(F32))


class Reduce:
    def __init__(self, me, own, theirs, halves, buffers, sums, cross, shares, outs, send, recv, free):
        self.me, self.own, self.theirs, self.halves, self.buffers = me, own, theirs, halves, buffers
        self.sums, self.cross, self.shares, self.outs, self.free = sums, cross, shares, outs, free
        self.copies = Copies(send, recv)
        self.waiting = set(range(6))
        self.streams = {(i, c): self.colour(i, c) for i in range(6) for c in range(3)} | {(i, 3): self.finish(i) for i in range(6)}

    def slot(self, i):
        kind, j = ORDER[i]
        return 0 if kind == TALL else j // 2

    def half(self, i):
        kind = ORDER[i][0]
        if i >= 3:
            pl.semaphore_wait(self.free.at[i - 3], sum(SIZES.values()) - len(SIZES) + 1)
        self.copies.start(
            (i, "half"), lambda: (self.halves[kind](), self.theirs[kind].at[self.slot(i)], self.me.device(core=1 - self.me.core))
        )

    def half_sent(self, i):
        self.copies.sent(lambda key: key == (i, "half"))

    def colour(self, i, c):
        kind, j = ORDER[i]
        slot = self.slot(i)
        if i in self.waiting:
            self.waiting.discard(i)
            self.copies.arrived((i, "half"))

        def last(colour, value):
            first, size = PART[kind][colour]
            if kind == WIDE:
                self.sums[WIDE][j, 0, :, first : first + size] = value[:4]
                self.sums[WIDE][j, 1, :, first : first + size] = value[4:]
            else:
                self.sums[TALL][j, first : first + size, :] = value

        grads = (lambda: self.own[kind].at[slot]), (lambda: self.theirs[kind].at[slot])
        yield from reduce_colour(self.me, self.copies, i, kind, c, grads, lambda c, p: self.buffers[kind, (c, p)].at[slot], last)

    def finish(self, i):
        (kind, j), me, copies = ORDER[i], self.me, self.copies
        sums, cross, shares, outs = self.sums, self.cross, self.shares, self.outs
        mine = 2 * lax.rem(me.at["z"], 2) + me.core
        if kind == WIDE:
            copies.start((i, "rows"), lambda: (sums[WIDE].at[j, 1 - me.core], cross[WIDE].at[j], me.device(core=1 - me.core)))
        else:
            for q in range(4):
                shares[j, q] = sums[TALL][j, 10 * q : 10 * q + 10, :]
            for o in range(3):

                def make(o=o):
                    z, core = ((me.at["z"], 1 - me.core), (me.pair(), me.core), (me.pair(), 1 - me.core))[o]
                    mine = 2 * lax.rem(me.at["z"], 2) + me.core
                    return shares.at[j, 2 * lax.rem(z, 2) + core], cross[TALL].at[j, mine], me.device(core=core, z=z)

                copies.start((i, "rows", o), make)
        if i < 3:
            for d, n in SIZES.items():
                each(n - 1, lambda o, d=d: self.done(i, me.device(**{d: me.off(d, o + 1)})))
            self.done(i, me.device(core=1 - me.core))
        yield
        mine = 2 * lax.rem(me.at["z"], 2) + me.core
        if kind == WIDE:
            copies.arrived((i, "rows"))
            outs[0][j, me.core] = sums[WIDE][j, me.core]
            outs[0][j, 1 - me.core] = cross[WIDE][j]
        else:
            for o in range(3):
                copies.arrived((i, "rows", o))
            for q in range(4):
                outs[1][j, q] = jnp.where(q == mine, shares[j, q], cross[TALL][j, q])
        copies.sent(lambda key: key[0] == i)

    def done(self, i, device):
        pl.semaphore_signal(self.free.at[i], inc=1, device_id=device, device_id_type=MESH)

    def run(self, order):
        for i, c in zip(order[::2], order[1::2], strict=True):
            if c == "h":
                self.half(int(i))
            elif c == "s":
                self.half_sent(int(i))
            else:
                next(self.streams[int(i), int(c)], None)


def dot(a, b, ca=1, cb=0):
    return lax.dot_general(a, b, (((ca,), (cb,)), ((), ())), preferred_element_type=F32)


def rem(a, b):
    return a % b if isinstance(a, int) else lax.rem(a, b)


def at_tile(i, size):
    return pl.ds(pl.multiple_of(i * size, size), size)


def put_rows(ref, i, value):
    y, z, rows = ref.shape[1:4]
    for s in range(0, 256, 8):
        row = i * 256 + s
        group = lax.div(row, rows)
        ref[lax.div(group, y * z), rem(lax.div(group, z), y), rem(group, z), pl.ds(pl.multiple_of(rem(row, rows), 8), 8), :] = value[s : s + 8]


def put_all(ref, value):
    ref[...] = value.reshape(ref.shape)


def backward_kernel(*refs):
    a1_in, dy_in, h1_in, a0_in, gate_in, up_in, w_gate, w_up, w_down = refs[:9]
    outs = refs[9:11]
    rest = list(refs[11:])
    take = lambda n: [rest.pop(0) for _ in range(n)]
    act, dy, turned, back, both, gates, ups, hidden = take(8)
    tile_g, tile_u, tile_d, rows_w = take(4)
    wide_own, wide_theirs, tall_own, tall_half, tall_theirs = take(5)
    wide_sums, tall_sums, wide_cross, tall_cross, shares = take(5)
    load, sem_g, sem_u, sem_d, sem_w, sem_f, send, recv, free = take(9)
    buffers = {}
    for kind in (WIDE, TALL):
        for k in reduce_buffers(kind):
            buffers[kind, k] = rest.pop(0)
    me = Me()

    def fetch(src, dst, sem):
        copy = pltpu.make_async_copy(src, dst, sem)
        copy.start()
        return copy

    class Stream:
        def __init__(self, tile, buffer, sem):
            self.tile, self.buffer, self.sem = tile, buffer, sem

        def copy(self, i):
            slot = rem(i, 2)
            return pltpu.make_async_copy(self.tile(i), self.buffer.at[slot], self.sem.at[slot])

    def stream(*streams, n):
        for s in streams:
            s.copy(0).start()

        def ahead(i):
            @pl.when(i + 1 < n)
            def _():
                for s in streams:
                    s.copy(i + 1).start()

            for s in streams:
                s.copy(i).wait()

        return ahead

    loads = [fetch(a1_in, act, load.at[0]), fetch(dy_in, dy, load.at[1])]
    first = stream(
        Stream(lambda i: w_gate.at[1, :, at_tile(i, 256)], tile_g, sem_g),
        Stream(lambda i: w_up.at[1, :, at_tile(i, 256)], tile_u, sem_u),
        Stream(lambda i: w_down.at[1, at_tile(i, 256), :], tile_d, sem_d),
        n=10,
    )
    me.barrier()
    own = {WIDE: wide_own, TALL: tall_own}
    theirs = {WIDE: wide_theirs, TALL: tall_theirs}
    halves = {WIDE: lambda: wide_own.at[2], TALL: lambda: tall_half}
    sums = {WIDE: wide_sums, TALL: tall_sums}
    cross = {WIDE: wide_cross, TALL: tall_cross}
    reduce = Reduce(me, own, theirs, halves, buffers, sums, cross, shares, outs, send, recv, free)

    def ticks(phase, i):
        orders = TICKS[phase]
        if any(orders):
            lax.switch(i, [functools.partial(reduce.run, order) for order in orders])

    def turn(src):
        @pl.loop(0, 8)
        def _(i):
            turned[:, at_tile(i, 128)] = src[at_tile(i, 128), :].T

    def unit(i, gate, up, dout):
        g, u, d = gate[...], up[...], hidden[...].astype(BF16).astype(F32)
        s = jax.nn.sigmoid(g)
        silu = g * s
        value = (silu * u).astype(BF16).T
        both[1, :, at_tile(i, 256)] = (d * silu).astype(BF16)
        both[0, :, at_tile(i, 256)] = (d * u * (s * (1 + g * (1 - s)))).astype(BF16)
        for ref, core in ((tall_own.at[0], me.core), (tall_half, 1 - me.core)):
            put_rows(ref, i, dot(value, dout[:, at_tile(core, 512)]).astype(BF16))

    def wide_grads(phase, layer):
        @pl.loop(0, 4)
        def _(k):
            which, mine = lax.div(k, 2), lax.rem(k, 2)
            core = mine * me.core + (1 - mine) * (1 - me.core)
            value = dot(turned[...], both[which, :, at_tile(core, 1280)]).astype(BF16)
            put_all(wide_own.at[lax.rem(2 - mine * (2 - which), 3)], value)
            ticks(phase, k)

    for copy in loads:
        copy.wait()
    turn(act)

    @pl.loop(0, 10)
    def _(i):
        first(i)
        unit(rem(i + 9, 10), gates.at[0], ups.at[0], dy)
        slot = lax.rem(i, 2)
        gates[0] = dot(act[...], tile_g[slot])
        ups[0] = dot(act[...], tile_u[slot])
        hidden[...] = dot(dy[...], tile_d[slot], 1, 1)

    unit(Me.zero + 9, gates.at[0], ups.at[0], dy)
    reduce.run(TICKS["first"][0])
    wide_grads("wide1", 1)

    load_h = fetch(h1_in, turned, load.at[0])

    def weight_rows(k, w):
        slot = rem(k, 2)
        rows = at_tile(k // 2 if isinstance(k, int) else lax.div(k, 2), 256)
        return pltpu.make_async_copy(w.at[1, rows, :], rows_w.at[slot], sem_w.at[slot])

    weight_rows(0, w_gate).start()

    @pl.loop(0, 8)
    def _(k):
        n, which = lax.div(k, 2), lax.rem(k, 2)

        @pl.when(which == 0)
        def _():
            weight_rows(k + 1, w_up).start()

        @pl.when((which == 1) & (k < 7))
        def _():
            weight_rows(k + 1, w_gate).start()

        weight_rows(k, w_gate).wait()
        part = dot(both[which], rows_w[which], 1, 1).astype(BF16).astype(F32)
        before = back[:, at_tile(n, 256)].astype(F32)
        back[:, at_tile(n, 256)] = (jnp.where(which == 0, 0.0, before) + part).astype(BF16)
        ticks("back", k)

    load_h.wait()

    @pl.loop(0, 8)
    def _(i):
        rows = at_tile(i, 128)
        h, d = turned[rows, :].astype(F32), back[rows, :].astype(F32)
        scale = lax.rsqrt(jnp.mean(h * h, -1, keepdims=True) + 1e-6)
        along = jnp.sum(d * h, -1, keepdims=True)
        d = (d * scale - h * (scale * scale * scale * along * (1 / 1024))).astype(BF16)
        act[rows, :] = (dy[rows, :].astype(F32) + d.astype(F32)).astype(BF16)

    load_a = fetch(a0_in, back, load.at[1])

    def gate_up(i):
        slot = rem(i, 2)
        return (
            pltpu.make_async_copy(gate_in.at[:, at_tile(i, 256)], gates.at[slot], sem_f.at[0, slot]),
            pltpu.make_async_copy(up_in.at[:, at_tile(i, 256)], ups.at[slot], sem_f.at[1, slot]),
        )

    second = stream(Stream(lambda i: w_down.at[0, at_tile(i, 256), :], tile_d, sem_d), n=10)
    load_a.wait()
    turn(back)

    @pl.loop(0, 10)
    def _(i):
        second(i)

        @pl.when(i > 0)
        def _():
            for copy in gate_up(i - 1):
                copy.wait()

        for copy in gate_up(i):
            copy.start()
        j = rem(i + 9, 10)
        unit(j, gates.at[lax.rem(j, 2)], ups.at[lax.rem(j, 2)], act)
        hidden[...] = dot(act[...], tile_d[lax.rem(i, 2)], 1, 1)
        ticks("units", i)

    for copy in gate_up(9):
        copy.wait()
    unit(Me.zero + 9, gates.at[1], ups.at[1], act)
    reduce.run(TICKS["last"][0])
    wide_grads("wide0", 0)
    reduce.run(TICKS["tail"][0])
    for stream_ in reduce.streams.values():
        assert next(stream_, 0) == 0, "not done"
    reduce.copies.sent()


def run(streams, order):
    for i, c in zip(order[::2], order[1::2], strict=True):
        next(streams[int(i), int(c)], None)
    for stream in streams.values():
        assert next(stream, 0) == 0, "not done"


def full_shape(kind):
    return dims(kind, ("x", "y", "z")) + (ROWS[kind], HALF[kind])


def backward(a1, dy, h1, a0, gate, up, w_gate, w_up, w_down):
    square = pltpu.VMEM((1024, 1024), BF16)
    scratch = [square] * 4 + [pltpu.VMEM((2, 1024, 2560), BF16)]
    scratch += [pltpu.VMEM((2, 1024, 256), F32)] * 2 + [pltpu.VMEM((1024, 256), F32)]
    scratch += [pltpu.VMEM((2, 1024, 256), BF16)] * 2 + [pltpu.VMEM((2, 256, 1024), BF16), pltpu.VMEM((2, 256, 2560), BF16)]
    scratch += [
        pltpu.VMEM((3, *full_shape(WIDE)), BF16),
        pltpu.VMEM((2, *full_shape(WIDE)), BF16),
        pltpu.VMEM((1, *full_shape(TALL)), BF16),
        pltpu.VMEM(full_shape(TALL), BF16),
        pltpu.VMEM((1, *full_shape(TALL)), BF16),
        pltpu.VMEM((4, 2, 4, 1280), F32),
        pltpu.VMEM((2, 40, 256), F32),
        pltpu.VMEM((4, 4, 1280), F32),
        pltpu.VMEM((2, 4, 10, 256), F32),
        pltpu.VMEM((2, 4, 10, 256), F32),
        *[pltpu.SemaphoreType.DMA((2,))] * 5,
        pltpu.SemaphoreType.DMA((2, 2)),
        pltpu.SemaphoreType.DMA((256,)),
        pltpu.SemaphoreType.DMA((256,)),
        pltpu.SemaphoreType.REGULAR((3,)),
    ]
    for kind, many in ((WIDE, 2), (TALL, 1)):
        scratch += [pltpu.VMEM((many, *shape), BF16) for shape in reduce_buffers(kind).values()]
    return pl.pallas_call(
        backward_kernel,
        out_shape=(jax.ShapeDtypeStruct((4, 2, 4, 1280), F32), jax.ShapeDtypeStruct((2, 4, 10, 256), F32)),
        in_specs=[pl.BlockSpec(memory_space=pl.ANY)] * 9,
        out_specs=(pl.BlockSpec(memory_space=pltpu.VMEM), pl.BlockSpec(memory_space=pltpu.VMEM)),
        scratch_shapes=scratch,
        compiler_params=pltpu.CompilerParams(collective_id=0, has_side_effects=True, vmem_limit_bytes=VMEM_LIMIT),
        name="backward",
    )(a1, dy, h1, a0, gate, up, w_gate, w_up, w_down)


def gather_colour(me, copies, key, kind, colour, ref):
    base = me.core * HALF[kind]
    fixed = dict(me.at)

    def part(at):
        return view(ref, kind, ("x", "y", "z"), at, colour, base)

    phases = COLOURS[colour][::-1]
    for phase, (d, how) in enumerate(phases):
        n, lastly = SIZES[d], phase == len(phases) - 1
        rest = {e: v for e, v in fixed.items() if e != d}
        here = part(fixed)

        def across(name, at):
            if lastly:
                copies.start((key, colour, "across", name), lambda: (part(at), part(at), me.device(core=1 - me.core)))

        if how == RING:
            long, short = lengths(n)
            ways = ((me.sign, long, "l"), (-me.sign, short, "s"))
            for s in range(long):
                for sign, length, name in ways:
                    if s >= length:
                        continue
                    at = {**rest, d: me.off(d, -sign * s)}
                    if s:
                        copies.arrived((key, colour, phase, name, s - 1))
                    copies.start(
                        (key, colour, phase, name, s),
                        lambda at=at, d=d, sign=sign: (part(at), part(at), me.device(**{d: me.off(d, sign)})),
                    )
                    if s:
                        across((name, s - 1), at)
                if s == 0:
                    across("own", fixed)
                yield
            for sign, length, name in ways:
                if length:
                    copies.arrived((key, colour, phase, name, length - 1))
                    across((name, length - 1), {**rest, d: me.off(d, -sign * length)})
        else:
            copies.start_all(
                (key, colour, phase), n - 1, lambda i, d=d, here=here: (here, here, me.device(**{d: me.off(d, i + 1)}))
            )
            yield
            copies.arrived((key, colour, phase))
        fixed = rest
    yield
    names = ["own"]
    d, how = phases[-1]
    long, short = lengths(SIZES[d])
    names += [("l", s) for s in range(long)] + [("s", s) for s in range(short)]
    for name in names:
        copies.arrived((key, colour, "across", name))


def gather_kernel(*refs):
    wide, tall, outs, rest = refs[0], refs[1], refs[2:8], refs[8:]
    cross = {WIDE: rest[0], TALL: rest[1]}
    forty, send, recv = rest[2:5]
    me = Me()
    me.barrier()
    copies = Copies(send, recv)
    mine = 2 * lax.rem(me.at["z"], 2) + me.core

    for i, (kind, j) in enumerate(ORDER):
        if kind == WIDE:
            copies.start((i, "rows"), lambda j=j: (wide.at[j, 1 - me.core], cross[WIDE].at[j], me.device(core=1 - me.core)))
        else:
            for o, (z, core) in enumerate(((me.at["z"], 1 - me.core), (me.pair(), me.core), (me.pair(), 1 - me.core))):
                q = 2 * lax.rem(z, 2) + core
                copies.start(
                    (i, "rows", o),
                    lambda j=j, q=q, z=z, core=core: (tall.at[j, q], cross[TALL].at[j, mine], me.device(core=core, z=z)),
                )

    def begin(i):
        kind, j = ORDER[i]
        here = view(outs[i], kind, ("x", "y", "z"), me.at, None, me.core * HALF[kind])
        if kind == WIDE:
            copies.arrived((i, "rows"))
            own, theirs = wide[j, me.core], cross[WIDE][j]
            first = me.core == 0
            rows = [jnp.where(first, own, theirs), jnp.where(first, theirs, own)]
            here[...] = jnp.concatenate(rows, axis=0).astype(BF16)
        else:
            for o in range(3):
                copies.arrived((i, "rows", o))
            for q in range(4):
                forty[10 * q : 10 * q + 10, :] = jnp.where(q == mine, tall[j, q], cross[TALL][j, q])
            here[...] = forty[...].astype(BF16)

    def colour(i, c):
        if i in waiting:
            waiting.discard(i)
            begin(i)
        yield from gather_colour(me, copies, i, ORDER[i][0], c, outs[i])

    waiting = set(range(6))
    run({(i, c): colour(i, c) for i in range(6) for c in range(3)}, GATHER_ORDER)
    copies.sent()


def all_gather(wide, tall):
    scratch = [
        pltpu.VMEM((4, 4, 1280), F32),
        pltpu.VMEM((2, 4, 10, 256), F32),
        pltpu.VMEM((40, 256), F32),
        pltpu.SemaphoreType.DMA((384,)),
        pltpu.SemaphoreType.DMA((384,)),
    ]
    return pl.pallas_call(
        gather_kernel,
        out_shape=tuple(pltpu.VMEM((*dims(kind, ("x", "y", "z")), ROWS[kind], 2 * HALF[kind]), BF16) for kind, _ in ORDER),
        in_specs=[pl.BlockSpec(memory_space=pltpu.VMEM)] * 2,
        out_specs=(pl.BlockSpec(memory_space=pltpu.VMEM),) * 6,
        scratch_shapes=scratch,
        compiler_params=pltpu.CompilerParams(collective_id=1, has_side_effects=True, vmem_limit_bytes=4 * 1024 * 1024),
        name="all_gather",
    )(wide, tall)


def spill_kernel(*refs):
    ins, outs, sem = refs[:6], refs[6:9], refs[9]
    copies = []
    for i, (kind, j) in enumerate(ORDER):
        which, layer = (2, j) if kind == TALL else (j // 2, j % 2)
        copies.append(pltpu.make_async_copy(ins[i], outs[which].at[layer], sem.at[i]))
        copies[-1].start()
    for copy in copies:
        copy.wait()


def spill(new):
    wide, tall = ((2, *dims(kind, ("x", "y", "z")), ROWS[kind], 2 * HALF[kind]) for kind in (WIDE, TALL))
    return pl.pallas_call(
        spill_kernel,
        out_shape=tuple(jax.ShapeDtypeStruct(shape, BF16) for shape in (wide, wide, tall)),
        in_specs=[pl.BlockSpec(memory_space=pltpu.VMEM)] * 6,
        out_specs=(pl.BlockSpec(memory_space=pl.ANY),) * 3,
        scratch_shapes=[pltpu.SemaphoreType.DMA((6,))],
        compiler_params=pltpu.CompilerParams(vmem_limit_bytes=1024 * 1024),
        name="spill",
    )(*new)


def normed(h):
    wide = h.astype(F32)
    scale = lax.rsqrt(jnp.mean(wide**2, -1, keepdims=True) + 1e-6)
    return (wide * scale).astype(BF16)


def adamw(w, m, v, g):
    m = 0.9 * m + 0.1 * g
    v = 0.95 * v + 0.05 * g * g
    step = m * lax.rsqrt(v + 1e-8) + 0.1 * w
    return (w - 0.02 * step).astype(BF16), m, v


def rows_of(wide, tall):
    wide = wide.transpose(0, 2, 1, 3).reshape(2, 2, 4, 2560)
    tall = tall.reshape(2, 2, 2, 10, 256).transpose(0, 3, 2, 1, 4).reshape(2, 10, 1024)
    return wide[0], wide[1], tall


def gathered(gate, up, down):
    wide = jnp.stack([gate, up]).reshape(4, 4, 2, 1280).transpose(0, 2, 1, 3).astype(F32)
    tall = down.reshape(2, 10, 2, 2, 256).transpose(0, 3, 2, 1, 4).reshape(2, 4, 10, 256).astype(F32)
    new = spill(all_gather(wide, tall))
    return tuple(w.reshape(2, -1, w.shape[-1]) for w in new)


def solution(mesh):
    def step(x, dy, *arrays):
        weights, m, v = (arrays[i : i + 3] for i in (0, 3, 6))
        w_gate, w_up, w_down = weights
        h0 = x[0]
        a0 = normed(h0)
        gate = jnp.dot(a0, w_gate[0], preferred_element_type=F32)
        up = jnp.dot(a0, w_up[0], preferred_element_type=F32)
        hidden = (jax.nn.silu(gate) * up).astype(BF16)
        h1 = h0 + jnp.dot(hidden, w_down[0], preferred_element_type=F32).astype(BF16)
        gradients = rows_of(*backward(normed(h1), dy[0], h1, a0, gate, up, w_gate, w_up, w_down))
        index = lax.axis_index("dp")
        news = []
        for w, mm, vv, g in zip(weights, m, v, gradients, strict=True):
            rows = mm.shape[1]
            mine = lax.dynamic_slice_in_dim(w, index * rows, rows, 1)
            news.append(adamw(mine.astype(F32), mm, vv, g))
        new = gathered(*(n[0] for n in news))
        return (*new, *(n[1] for n in news), *(n[2] for n in news))

    batch, whole, rows = P(("rep", "dp")), P(), P(None, "dp")
    return jax.shard_map(
        step,
        mesh=mesh,
        in_specs=(batch, batch, *(whole,) * 3, *(rows,) * 6),
        out_specs=(*(P("rep"),) * 3, *(P("rep", "dp"),) * 6),
        check_vma=False,
    )
```

profile of v0, /device:TPU:1, one launch (start us, length us, event | category | flops | bytes accessed | tf_op | source)
XLA Modules:
  0.0 318.5 jit_solution(18118432606286606554)
XLA Ops:
  0.6 0.0 copy-start
  0.7 2.2 fusion.9
  2.9 1.6 constant_dynamic-slice_fusion
  4.4 0.0 slice-start.3
  4.4 3.5 %fusion.10.refs_3_ = bf16[1024,1024]{1,0:T(8,128)(2,1)} fusion(bf16[1,1024,1024]{2,1,0:T(8,128)(2,1)} %param.11, f32[1024]{0:T(1024)S(1)} %add_rsqrt_fusion.1), kind=kLoop, calls=%fused_computation.15 | loop fusion | flops 3145728 | bytes 4198400 | tf_op jit(solution)/shard_map/convert_element_type | solution.py:728
  7.9 0.0 copy-done
  7.9 0.0 slice-start.4
  7.9 0.0 slice-start.5
  7.9 0.0 slice-start
  7.9 0.0 slice-start.1
  7.9 11.0 %fusion.2.refs_5_ = f32[1024,2560]{1,0:T(8,128)} fusion(bf16[2,1024,2560]{2,1,0:T(8,128)(2,1)} %refs_7_.1, bf16[1,1024,1024]{2,1,0:T(8,128)(2,1)S(1)} %copy-done, f32[1024]{0:T(1024)S(1)} %add_rsqrt_fusion.1), kind=kOutput, calls=%fused_computation.7 | convolution fusion | flops 5371854848 | bytes 17829888 | tf_op jit(solution)/shard_map/dot_general | solution.py:758
  19.0 0.0 slice-done.3
  19.0 0.0 slice-done.4
  19.0 0.0 slice-done.5
  19.0 0.0 slice-start.2
  19.0 8.3 %fusion.4.refs_4_ = f32[1024,2560]{1,0:T(8,128)} fusion(bf16[2,1024,2560]{2,1,0:T(8,128)(2,1)S(1)} %bitcast.50, bf16[1,1024,1024]{2,1,0:T(8,128)(2,1)S(1)} %copy-done, f32[1024]{0:T(1024)S(1)} %add_rsqrt_fusion.1), kind=kOutput, calls=%fused_computation.9 | convolution fusion | flops 5371854848 | bytes 17829888 | tf_op jit(solution)/shard_map/dot_general | solution.py:757
  27.2 0.0 slice-done
  27.2 0.0 slice-done.1
  27.2 0.0 slice-done.2
  27.3 10.6 %fusion.11 = (f32[1024]{0:T(1024)S(1)}, bf16[1024,1024]{1,0:T(8,128)(2,1)S(1)}) fusion(bf16[2,2560,1024]{2,1,0:T(8,128)(2,1)S(1)} %bitcast.48, f32[1024,2560]{1,0:T(8,128)} %fusion.2.refs_5_, f32[1024,2560]{1,0:T(8,128)} %fusion.4.refs_4_, bf16[1,1024,1024]{2,1,0:T(8,128)(2,1)S(1)} %copy-done), kind=kOutput, calls=%fused_computation.16 | convolution fusion | flops 5389679616 | bytes 30412800 | tf_op jit(solution)/shard_map/dot_general | solution.py:760
  37.8 0.0 copy-start.1
  37.9 1.3 copy-done.1
  39.2 1.7 fusion.12.refs_0_
  40.9 176.6 %backward.1 = (f32[4,2,4,1280]{3,2,1,0:T(4,128)}, f32[2,4,10,256]{3,2,1,0:T(8,128)}) custom-call(bf16[1024,1024]{1,0:T(8,128)(2,1)} %fusion.12.refs_0_, bf16[1024,1024]{1,0:T(8,128)(2,1)} %bitcast.51, bf16[1024,1024]{1,0:T(8,128)(2,1)} %copy-done.1, bf16[1024,1024]{1,0:T(8,128)(2,1)} %fusion.10.refs_3_, f32[1024,2560]{1,0:T(8,128)} %fusion.4.refs_4_, ...), custom_call_target="tpu_custom_call" | custom-call | tf_op jit(solution)/shard_map/backward/pallas_call | solution.py:568
  217.5 1.0 copy.22
  218.5 0.1 reshape.80
  218.6 0.9 fusion.37
  219.5 1.8 fusion.32
  221.4 0.1 reshape.86
  221.5 2.0 fusion.30
  223.5 0.1 pad_maximum_fusion
  223.6 84.3 %all_gather.1 = (bf16[4,4,4,40,1024]{4,3,2,1,0:T(8,128)(2,1)S(1)}, bf16[4,4,8,8,2560]{4,3,2,1,0:T(8,128)(2,1)S(1)}, bf16[4,4,8,8,2560]{4,3,2,1,0:T(8,128)(2,1)S(...) custom-call(f32[4,2,4,1280]{3,2,1,0:T(4,128)S(1)} %convert_bitcast_f, ...), custom_call_target="tpu_custom_call" | custom-call | tf_op jit(solution)/shard_map/all_gather/pallas_call | solution.py:690
  307.9 10.4 %spill.1 = (bf16[2,4,4,8,8,2560]{5,4,3,2,1,0:T(8,128)(2,1)}, bf16[2,4,4,8,8,2560]{5,4,3,2,1,0:T(8,128)(2,1)}, bf16[2,4,4,4,40,1024]{5,4,3,2,1,0:T(8,128)(2,1)}) custom-call(bf16[4,4,4,40,1024]{4,3,2,1,0:T(8,128)(2,1)S(1)} %get-tuple-element.22.refs_0_, bf16[4,4,8,8,2560]{4,3,2,1,0:T(8,128)(2,1)S(1)} %get-tuple-element.23.refs_1_, ...), custom_call_target="tpu_custom_call" | custom-call | tf_op jit(solution)/shard_map/spill/pallas_call | solution.py:714
  (6 shorter events, 0.1 us)
Async XLA Ops:
  0.6 7.3 %copy-start = (bf16[1,1024,1024]{2,1,0:T(8,128)(2,1)S(1)}, bf16[1,1024,1024]{2,1,0:T(8,128)(2,1)}, u32[]{:S(2)}) copy-start(bf16[1,1024,1024]{2,1,0:T(8,128)(2,1)} %param.11) | copy-start | bytes 6291460
  4.4 14.5 %slice-start.3 = ((s8[10485760]{0:T(1024)(128)(4,1)}), s8[4194304]{0:T(1024)(128)(4,1)S(1)}, s32[]{:S(2)}) async-start(s8[10485760]{0:T(1024)(128)(4,1)} %bitcast.49), calls=%async_computation.3 | async-start | bytes 8388608
  7.9 11.0 %slice-start.4 = ((s8[10485760]{0:T(1024)(128)(4,1)}), s8[4194304]{0:T(1024)(128)(4,1)S(1)}, s32[]{:S(2)}) async-start(s8[10485760]{0:T(1024)(128)(4,1)} %bitcast.49), calls=%async_computation.4 | async-start | bytes 8388608
  7.9 11.0 %slice-start.5 = ((s8[10485760]{0:T(1024)(128)(4,1)}), s8[2097152]{0:T(1024)(128)(4,1)S(1)}, s32[]{:S(2)}) async-start(s8[10485760]{0:T(1024)(128)(4,1)} %bitcast.49), calls=%async_computation.5 | async-start | bytes 4194304
  7.9 19.3 %slice-start = ((s8[10485760]{0:T(1024)(128)(4,1)}), s8[4194304]{0:T(1024)(128)(4,1)S(1)}, s32[]{:S(2)}) async-start(s8[10485760]{0:T(1024)(128)(4,1)} %bitcast.47), calls=%async_computation | async-start | bytes 8388608
  7.9 19.3 %slice-start.1 = ((s8[10485760]{0:T(1024)(128)(4,1)}), s8[4194304]{0:T(1024)(128)(4,1)S(1)}, s32[]{:S(2)}) async-start(s8[10485760]{0:T(1024)(128)(4,1)} %bitcast.47), calls=%async_computation.1 | async-start | bytes 8388608
  19.0 8.3 %slice-start.2 = ((s8[10485760]{0:T(1024)(128)(4,1)}), s8[2097152]{0:T(1024)(128)(4,1)S(1)}, s32[]{:S(2)}) async-start(s8[10485760]{0:T(1024)(128)(4,1)} %bitcast.47), calls=%async_computation.2 | async-start | bytes 4194304
  37.8 1.3 copy-start.1
where the time goes:
time: 319 us
  Pallas kernels  271 us (85%)
  matrix products  29.8 us (9%)
  other arithmetic  11.3 us (4%)
  local copies, waits for them, and re-layouts  5.04 us (2%)
    pallas_call x1, Pallas kernels, backward(): pl.pallas_call(backward_kernel, out_shape=(jax.ShapeDtypeStruct((4, 2, 4,...  177 us
    pallas_call x1, Pallas kernels, all_gather(): pl.pallas_call(gather_kernel, out_shape=tuple((pltpu.VMEM((*dims(kind, ('...  84.3 us
    dot_general x1, matrix products, step(): up = jnp.dot(a0, w_up[0], preferred_element_type=F32)  11 us
    dot_general x1, matrix products, step(): jnp.dot(hidden, w_down[0], preferred_element_type=F32).astype(BF16)  10.6 us
    pallas_call x1, Pallas kernels, spill(): pl.pallas_call(spill_kernel, out_shape=tuple((jax.ShapeDtypeStruct(shape,...  10.4 us
    dot_general x1, matrix products, step(): gate = jnp.dot(a0, w_gate[0], preferred_element_type=F32)  8.25 us

commit v1 on v0

--- a/solution.py
+++ b/solution.py
@@ -15,14 +15,14 @@
 
 TICKS = {
     "first": ["0h"],
-    "wide1": ["1h", "1s", "2h020100", "12110210222120"],
-    "back": ["", "01001202", "111022", "", "122120010002", "111022", "1202210020", "0111102202001221200111021022202112000103221112101303"],
-    "units": ["1321202223", "", "23", "", "", "", "", "", "", ""],
+    "wide1": ["1h", "1s020100", "2h", "02121110"],
+    "back": ["010022212002", "", "121110", "22", "02", "0100122120", "11220210", "010012212010110201001211100222212012012120000311221210131303"],
+    "units": ["222120", "", "2223", "23", "", "", "", "", "", ""],
     "last": ["3h"],
-    "wide0": ["4h", "4s", "5h323130", "42413240525150"],
-    "tail": ["3130423241405242515032313052414042513230504031415251304231324140505251324230503133524142404351334352505353"],
+    "wide0": ["4h", "4s323130", "5h", "32424140"],
+    "tail": ["3130525150324241405232313042515052414032303151424050413032523151404241503251305250423133404252414333514350525353"],
 }
-GATHER_ORDER = "020100121110222120023231301242412240013202525150004211125210220121002032104211003120300110215241110240203051501200310122321011214240413050520220511201110122001132213140500010414210522102302112203151222032414042525002021231302212323140514230223252414050425241515051"
+GATHER_ORDER = "020100121110222120323102304212414022525101325002420052121110220100212032104200311152200130102141402051025000123101113022403250102142410152200201511112300040315000222110324110421111205251200231123022213240214241505202510212302212313230402242314132405042524151505251"
 
 
 RING, DIRECT = "ring", "direct"
@@ -347,16 +347,16 @@
     ref[...] = value.reshape(ref.shape)
 
 
-def backward_kernel(*refs):
-    a1_in, dy_in, h1_in, a0_in, gate_in, up_in, w_gate, w_up, w_down = refs[:9]
-    outs = refs[9:11]
+def step_kernel(*refs):
+    x_in, dy_in, w_gate, w_up, w_down = refs[:5]
+    outs, (gate_kept, up_kept, a0_kept, h1_kept) = refs[5:7], refs[7:11]
     rest = list(refs[11:])
     take = lambda n: [rest.pop(0) for _ in range(n)]
-    act, dy, turned, back, both, gates, ups, hidden = take(8)
-    tile_g, tile_u, tile_d, rows_w = take(4)
+    act, dy, turned, back, both, gates, ups = take(7)
+    tile_g, tile_u, tile_d, rows_w, columns_w = take(5)
     wide_own, wide_theirs, tall_own, tall_half, tall_theirs = take(5)
     wide_sums, tall_sums, wide_cross, tall_cross, shares = take(5)
-    load, sem_g, sem_u, sem_d, sem_w, sem_f, send, recv, free = take(9)
+    load, sem_g, sem_u, sem_d, sem_w, sem_c, sem_f, send, recv, free = take(10)
     buffers = {}
     for kind in (WIDE, TALL):
         for k in reduce_buffers(kind):
@@ -391,13 +391,12 @@
 
         return ahead
 
-    loads = [fetch(a1_in, act, load.at[0]), fetch(dy_in, dy, load.at[1])]
-    first = stream(
-        Stream(lambda i: w_gate.at[1, :, at_tile(i, 256)], tile_g, sem_g),
-        Stream(lambda i: w_up.at[1, :, at_tile(i, 256)], tile_u, sem_u),
-        Stream(lambda i: w_down.at[1, at_tile(i, 256), :], tile_d, sem_d),
-        n=10,
-    )
+    def columns(w, layer, buffer, sem):
+        return Stream(lambda i: w.at[layer, :, at_tile(i, 256)], buffer, sem)
+
+    loads = [fetch(x_in, back, load.at[0]), fetch(dy_in, dy, load.at[1])]
+    zeroth = stream(columns(w_gate, 0, tile_g, sem_g), columns(w_up, 0, tile_u, sem_u), n=10)
+    down = stream(columns(w_down, 0, columns_w, sem_c), n=4)
     me.barrier()
     own = {WIDE: wide_own, TALL: tall_own}
     theirs = {WIDE: wide_theirs, TALL: tall_theirs}
@@ -411,13 +410,20 @@
         if any(orders):
             lax.switch(i, [functools.partial(reduce.run, order) for order in orders])
 
+    def norm():
+        @pl.loop(0, 8)
+        def _(i):
+            rows = at_tile(i, 128)
+            h = back[rows, :].astype(F32)
+            act[rows, :] = (h * lax.rsqrt(jnp.mean(h * h, -1, keepdims=True) + 1e-6)).astype(BF16)
+
     def turn(src):
         @pl.loop(0, 8)
         def _(i):
             turned[:, at_tile(i, 128)] = src[at_tile(i, 128), :].T
 
-    def unit(i, gate, up, dout):
-        g, u, d = gate[...], up[...], hidden[...].astype(BF16).astype(F32)
+    def unit(i, g, u, d, dout):
+        d = d.astype(BF16).astype(F32)
         s = jax.nn.sigmoid(g)
         silu = g * s
         value = (silu * u).astype(BF16).T
@@ -426,7 +432,7 @@
         for ref, core in ((tall_own.at[0], me.core), (tall_half, 1 - me.core)):
             put_rows(ref, i, dot(value, dout[:, at_tile(core, 512)]).astype(BF16))
 
-    def wide_grads(phase, layer):
+    def wide_grads(phase):
         @pl.loop(0, 4)
         def _(k):
             which, mine = lax.div(k, 2), lax.rem(k, 2)
@@ -435,24 +441,65 @@
             put_all(wide_own.at[lax.rem(2 - mine * (2 - which), 3)], value)
             ticks(phase, k)
 
+    def kept(i, out):
+        slot = rem(i, 2)
+        pairs = (gates.at[slot], gate_kept.at[:, at_tile(i, 256)]), (ups.at[slot], up_kept.at[:, at_tile(i, 256)])
+        return [pltpu.make_async_copy(*(p if out else p[::-1]), sem_f.at[n, slot]) for n, p in enumerate(pairs)]
+
     for copy in loads:
         copy.wait()
+    norm()
+    keep = fetch(act, a0_kept, load.at[0])
+
+    @pl.loop(0, 10)
+    def _(i):
+        zeroth(i)
+
+        @pl.when(i >= 2)
+        def _():
+            for copy in kept(i - 2, True):
+                copy.wait()
+
+        slot = rem(i, 2)
+        g, u = dot(act[...], tile_g[slot]), dot(act[...], tile_u[slot])
+        gates[slot] = g
+        ups[slot] = u
+        both[0, :, at_tile(i, 256)] = (g * jax.nn.sigmoid(g) * u).astype(BF16)
+        for copy in kept(i, True):
+            copy.start()
+
+    first = stream(
+        columns(w_gate, 1, tile_g, sem_g),
+        columns(w_up, 1, tile_u, sem_u),
+        Stream(lambda i: w_down.at[1, at_tile(i, 256), :], tile_d, sem_d),
+        n=10,
+    )
+
+    @pl.loop(0, 4)
+    def _(i):
+        down(i)
+        part = dot(both[0], columns_w[rem(i, 2)]).astype(BF16).astype(F32)
+        back[:, at_tile(i, 256)] = (back[:, at_tile(i, 256)].astype(F32) + part).astype(BF16)
+
+    keep.wait()
+    keep = fetch(back, h1_kept, load.at[0])
+    norm()
     turn(act)
 
     @pl.loop(0, 10)
     def _(i):
         first(i)
-        unit(rem(i + 9, 10), gates.at[0], ups.at[0], dy)
-        slot = lax.rem(i, 2)
-        gates[0] = dot(act[...], tile_g[slot])
-        ups[0] = dot(act[...], tile_u[slot])
-        hidden[...] = dot(dy[...], tile_d[slot], 1, 1)
-
-    unit(Me.zero + 9, gates.at[0], ups.at[0], dy)
+        slot = rem(i, 2)
+        unit(i, dot(act[...], tile_g[slot]), dot(act[...], tile_u[slot]), dot(dy[...], tile_d[slot], 1, 1), dy)
+
     reduce.run(TICKS["first"][0])
-    wide_grads("wide1", 1)
-
-    load_h = fetch(h1_in, turned, load.at[0])
+    wide_grads("wide1")
+
+    keep.wait()
+    for i in (8, 9):
+        for copy in kept(i, True):
+            copy.wait()
+    load_h = fetch(h1_kept, turned, load.at[0])
 
     def weight_rows(k, w):
         slot = rem(k, 2)
@@ -490,40 +537,29 @@
         d = (d * scale - h * (scale * scale * scale * along * (1 / 1024))).astype(BF16)
         act[rows, :] = (dy[rows, :].astype(F32) + d.astype(F32)).astype(BF16)
 
-    load_a = fetch(a0_in, back, load.at[1])
-
-    def gate_up(i):
-        slot = rem(i, 2)
-        return (
-            pltpu.make_async_copy(gate_in.at[:, at_tile(i, 256)], gates.at[slot], sem_f.at[0, slot]),
-            pltpu.make_async_copy(up_in.at[:, at_tile(i, 256)], ups.at[slot], sem_f.at[1, slot]),
-        )
-
+    load_a = fetch(a0_kept, back, load.at[1])
     second = stream(Stream(lambda i: w_down.at[0, at_tile(i, 256), :], tile_d, sem_d), n=10)
+    for copy in kept(0, False):
+        copy.start()
     load_a.wait()
     turn(back)
 
     @pl.loop(0, 10)
     def _(i):
+        @pl.when(i < 9)
+        def _():
+            for copy in kept(i + 1, False):
+                copy.start()
+
         second(i)
-
-        @pl.when(i > 0)
-        def _():
-            for copy in gate_up(i - 1):
-                copy.wait()
-
-        for copy in gate_up(i):
-            copy.start()
-        j = rem(i + 9, 10)
-        unit(j, gates.at[lax.rem(j, 2)], ups.at[lax.rem(j, 2)], act)
-        hidden[...] = dot(act[...], tile_d[lax.rem(i, 2)], 1, 1)
+        for copy in kept(i, False):
+            copy.wait()
+        slot = rem(i, 2)
+        unit(i, gates[slot], ups[slot], dot(act[...], tile_d[slot], 1, 1), act)
         ticks("units", i)
 
-    for copy in gate_up(9):
-        copy.wait()
-    unit(Me.zero + 9, gates.at[1], ups.at[1], act)
     reduce.run(TICKS["last"][0])
-    wide_grads("wide0", 0)
+    wide_grads("wide0")
     reduce.run(TICKS["tail"][0])
     for stream_ in reduce.streams.values():
         assert next(stream_, 0) == 0, "not done"
@@ -541,12 +577,13 @@
     return dims(kind, ("x", "y", "z")) + (ROWS[kind], HALF[kind])
 
 
-def backward(a1, dy, h1, a0, gate, up, w_gate, w_up, w_down):
+def summed(x, dy, w_gate, w_up, w_down):
     square = pltpu.VMEM((1024, 1024), BF16)
     scratch = [square] * 4 + [pltpu.VMEM((2, 1024, 2560), BF16)]
-    scratch += [pltpu.VMEM((2, 1024, 256), F32)] * 2 + [pltpu.VMEM((1024, 256), F32)]
+    scratch += [pltpu.VMEM((2, 1024, 256), F32)] * 2
     scratch += [pltpu.VMEM((2, 1024, 256), BF16)] * 2 + [pltpu.VMEM((2, 256, 1024), BF16), pltpu.VMEM((2, 256, 2560), BF16)]
     scratch += [
+        pltpu.VMEM((2, 2560, 256), BF16),
         pltpu.VMEM((3, *full_shape(WIDE)), BF16),
         pltpu.VMEM((2, *full_shape(WIDE)), BF16),
         pltpu.VMEM((1, *full_shape(TALL)), BF16),
@@ -557,7 +594,7 @@
         pltpu.VMEM((4, 4, 1280), F32),
         pltpu.VMEM((2, 4, 10, 256), F32),
         pltpu.VMEM((2, 4, 10, 256), F32),
-        *[pltpu.SemaphoreType.DMA((2,))] * 5,
+        *[pltpu.SemaphoreType.DMA((2,))] * 6,
         pltpu.SemaphoreType.DMA((2, 2)),
         pltpu.SemaphoreType.DMA((256,)),
         pltpu.SemaphoreType.DMA((256,)),
@@ -565,15 +602,16 @@
     ]
     for kind, many in ((WIDE, 2), (TALL, 1)):
         scratch += [pltpu.VMEM((many, *shape), BF16) for shape in reduce_buffers(kind).values()]
+    kept = [jax.ShapeDtypeStruct((1024, 2560), F32)] * 2 + [jax.ShapeDtypeStruct((1024, 1024), BF16)] * 2
     return pl.pallas_call(
-        backward_kernel,
-        out_shape=(jax.ShapeDtypeStruct((4, 2, 4, 1280), F32), jax.ShapeDtypeStruct((2, 4, 10, 256), F32)),
-        in_specs=[pl.BlockSpec(memory_space=pl.ANY)] * 9,
-        out_specs=(pl.BlockSpec(memory_space=pltpu.VMEM), pl.BlockSpec(memory_space=pltpu.VMEM)),
+        step_kernel,
+        out_shape=(jax.ShapeDtypeStruct((4, 2, 4, 1280), F32), jax.ShapeDtypeStruct((2, 4, 10, 256), F32), *kept),
+        in_specs=[pl.BlockSpec(memory_space=pl.ANY)] * 5,
+        out_specs=(*[pl.BlockSpec(memory_space=pltpu.VMEM)] * 2, *[pl.BlockSpec(memory_space=pl.ANY)] * 4),
         scratch_shapes=scratch,
         compiler_params=pltpu.CompilerParams(collective_id=0, has_side_effects=True, vmem_limit_bytes=VMEM_LIMIT),
-        name="backward",
-    )(a1, dy, h1, a0, gate, up, w_gate, w_up, w_down)
+        name="step",
+    )(x, dy, w_gate, w_up, w_down)[:2]
 
 
 def gather_colour(me, copies, key, kind, colour, ref):
@@ -722,12 +760,6 @@
     )(*new)
 
 
-def normed(h):
-    wide = h.astype(F32)
-    scale = lax.rsqrt(jnp.mean(wide**2, -1, keepdims=True) + 1e-6)
-    return (wide * scale).astype(BF16)
-
-
 def adamw(w, m, v, g):
     m = 0.9 * m + 0.1 * g
     v = 0.95 * v + 0.05 * g * g
@@ -751,14 +783,7 @@
 def solution(mesh):
     def step(x, dy, *arrays):
         weights, m, v = (arrays[i : i + 3] for i in (0, 3, 6))
-        w_gate, w_up, w_down = weights
-        h0 = x[0]
-        a0 = normed(h0)
-        gate = jnp.dot(a0, w_gate[0], preferred_element_type=F32)
-        up = jnp.dot(a0, w_up[0], preferred_element_type=F32)
-        hidden = (jax.nn.silu(gate) * up).astype(BF16)
-        h1 = h0 + jnp.dot(hidden, w_down[0], preferred_element_type=F32).astype(BF16)
-        gradients = rows_of(*backward(normed(h1), dy[0], h1, a0, gate, up, w_gate, w_up, w_down))
+        gradients = rows_of(*summed(x[0], dy[0], *weights))
         index = lax.axis_index("dp")
         news = []
         for w, mm, vv, g in zip(weights, m, v, gradients, strict=True):

time: 319 us -> 296 us (0.928)
  matrix products: 29.8 us -> 0 us
  Pallas kernels: 271 us -> 287 us
  other arithmetic: 11.3 us -> 3.9 us
    dot_general x3 -> x0, matrix products: 29.8 us -> none  [the longest x1 11 us: step(): up = jnp.dot(a0, w_up[0], preferred_element_type=F32)]
    pallas_call x1, Pallas kernels: 177 us -> 194 us  [summed(): pl.pallas_call(step_kernel, out_shape=(jax.ShapeDtypeStruct((4, 2, 4, 128...]
    convert_element_type x2 -> x0, other arithmetic: 5.19 us -> none  [normed(): return (wide * scale).astype(BF16)]
where the time goes in v1:
time: 296 us; the launch traced here: 295 us
  Pallas kernels  287 us (97%)
  other arithmetic  3.9 us (1%)
  local copies, waits for them, and re-layouts  3.69 us (1%)
    pallas_call x1, Pallas kernels, summed(): pl.pallas_call(step_kernel, out_shape=(jax.ShapeDtypeStruct((4, 2, 4, 128...  194 us
    pallas_call x1, Pallas kernels, all_gather(): pl.pallas_call(gather_kernel, out_shape=tuple((pltpu.VMEM((*dims(kind, ('...  82.2 us
    pallas_call x1, Pallas kernels, spill(): pl.pallas_call(spill_kernel, out_shape=tuple((jax.ShapeDtypeStruct(shape,...  10.4 us

profile of v1, /device:TPU:1, one launch (start us, length us, event | category | flops | bytes accessed | tf_op | source)
XLA Modules:
  0.0 295.5 jit_solution(2455855902124018368)
XLA Ops:
  0.6 1.6 constant_dynamic-slice_fusion
  2.2 194.3 %step.1 = (f32[4,2,4,1280]{3,2,1,0:T(4,128)}, f32[2,4,10,256]{3,2,1,0:T(8,128)}, f32[1024,2560]{1,0:T(8,128)}, f32[1024,2560]{1,0:T(8,128)}, bf16[1024,1024]{1,0:T(8,128)(2,1)}, /*index=5*/bf16[1024,1024]{1,0:T(8,128)(2,1)}) custom-call(bf16[1024,1024]{1,0:T(8,128)(2,1)} %bitcast.27, bf16[1024,1024]{1,0:T(8,128)(2,1)} %bitcast.28, ...), custom_call_target="tpu_custom_call" | custom-call | tf_op jit(solution)/shard_map/step/pallas_call | solution.py:606
  196.5 1.0 copy.21
  197.5 0.1 reshape.48
  197.6 0.9 fusion.18
  198.6 1.8 fusion.14
  200.4 0.1 reshape.54
  200.5 2.0 fusion.12
  202.5 0.1 pad_maximum_fusion
  202.6 82.2 %all_gather.1 = (bf16[4,4,4,40,1024]{4,3,2,1,0:T(8,128)(2,1)S(1)}, bf16[4,4,8,8,2560]{4,3,2,1,0:T(8,128)(2,1)S(1)}, bf16[4,4,8,8,2560]{4,3,2,1,0:T(8,128)(2,1)S(...) custom-call(f32[4,2,4,1280]{3,2,1,0:T(4,128)S(1)} %convert_bitcast_f, ...), custom_call_target="tpu_custom_call" | custom-call | tf_op jit(solution)/shard_map/all_gather/pallas_call | solution.py:728
  284.9 10.4 %spill.1 = (bf16[2,4,4,8,8,2560]{5,4,3,2,1,0:T(8,128)(2,1)}, bf16[2,4,4,8,8,2560]{5,4,3,2,1,0:T(8,128)(2,1)}, bf16[2,4,4,4,40,1024]{5,4,3,2,1,0:T(8,128)(2,1)}) custom-call(bf16[4,4,4,40,1024]{4,3,2,1,0:T(8,128)(2,1)S(1)} %get-tuple-element.22.refs_0_, bf16[4,4,8,8,2560]{4,3,2,1,0:T(8,128)(2,1)S(1)} %get-tuple-element.23.refs_1_, ...), custom_call_target="tpu_custom_call" | custom-call | tf_op jit(solution)/shard_map/spill/pallas_call | solution.py:752
  (2 shorter events, 0.0 us)

commit v2 on v1

--- a/solution.py
+++ b/solution.py
@@ -15,14 +15,14 @@
 
 TICKS = {
     "first": ["0h"],
-    "wide1": ["1h", "1s020100", "2h", "02121110"],
-    "back": ["010022212002", "", "121110", "22", "02", "0100122120", "11220210", "010012212010110201001211100222212012012120000311221210131303"],
-    "units": ["222120", "", "2223", "23", "", "", "", "", "", ""],
+    "wide1": ["1h", "1s020100", "2h121110", "0200"],
+    "back": ["0112222120", "", "02111000", "12", "0122", "022120", "121100", "01102221020s"],
+    "units": ["010012021110222120", "", "0211121021222001", "0003", "122022", "03111013", "132221", "2023", "23", ""],
     "last": ["3h"],
-    "wide0": ["4h", "4s323130", "5h", "32424140"],
-    "tail": ["3130525150324241405232313042515052414032303151424050413032523151404241503251305250423133404252414333514350525353"],
+    "wide0": ["4h", "4s323130", "5h424140", "3230"],
+    "tail": ["42523151504041324230523150325142413040315251323042405041523151403050324142515250324231335240414333514350525353"],
 }
-GATHER_ORDER = "020100121110222120323102304212414022525101325002420052121110220100212032104200311152200130102141402051025000123101113022403250102142410152200201511112300040315000222110324110421111205251200231123022213240214241505202510212302212313230402242314132405042524151505251"
+GATHER_ORDER = "020100121110222120323130424140525150021222324252010011021000122122203210420031520130112120411040300051203150014002301121124150223210014240005251000211122120225031323001414201115211100210214012512122203132422052500241301202302251124022324240313252425031524150415151"
 
 
 RING, DIRECT = "ring", "direct"
@@ -32,7 +32,7 @@
     (("z", RING), ("x", DIRECT), ("y", DIRECT)),
 )
 WIDE, TALL = "wide", "tall"
-PART = {WIDE: ((0, 384), (384, 384), (768, 512)), TALL: ((0, 16), (16, 16), (32, 8))}
+PART = {WIDE: ((0, 512), (512, 384), (896, 384)), TALL: ((0, 8), (8, 16), (24, 16))}
 HALF = {WIDE: 1280, TALL: 512}
 ROWS = {WIDE: 8, TALL: 40}
 ORDER = ((TALL, 1), (WIDE, 1), (WIDE, 3), (TALL, 0), (WIDE, 0), (WIDE, 2))
@@ -175,7 +175,7 @@
     return functools.reduce(jnp.add, [p[...].astype(F32) for p in parts])
 
 
-def reduce_colour(me, copies, key, kind, colour, grads, received, last):
+def reduce_colour(me, copies, key, kind, colour, grads, received, last, keep=None):
     free, fixed = ("x", "y", "z"), {}
     parts = [lambda at, r=r: view(r(), kind, ("x", "y", "z"), at, colour) for r in grads]
     out = parts[0]
@@ -232,13 +232,19 @@
             copies.arrived((key, colour, phase))
             parts = parts + [slot(i) for i in range(n - 1)]
         fixed = {**fixed, d: me.at[d]}
+        if keep is not None and phase == 0:
+            copies.sent(lambda k: k[:3] == (key, colour, 0))
+            stays = (lambda at, left=left: view(keep, kind, left, {e: v for e, v in at.items() if e in left}, colour, own=True))
+            stays(fixed)[...] = out(fixed)[...]
+            out = stays
+            parts[0] = stays
     last(colour, total([p(fixed) for p in parts]).astype(BF16).astype(F32))
 
 
 class Reduce:
-    def __init__(self, me, own, theirs, halves, buffers, sums, cross, shares, outs, send, recv, free):
+    def __init__(self, me, own, theirs, halves, buffers, sums, cross, shares, outs, send, recv, free, kept):
         self.me, self.own, self.theirs, self.halves, self.buffers = me, own, theirs, halves, buffers
-        self.sums, self.cross, self.shares, self.outs, self.free = sums, cross, shares, outs, free
+        self.sums, self.cross, self.shares, self.outs, self.free, self.kept = sums, cross, shares, outs, free, kept
         self.copies = Copies(send, recv)
         self.waiting = set(range(6))
         self.streams = {(i, c): self.colour(i, c) for i in range(6) for c in range(3)} | {(i, 3): self.finish(i) for i in range(6)}
@@ -274,7 +280,8 @@
                 self.sums[TALL][j, first : first + size, :] = value
 
         grads = (lambda: self.own[kind].at[slot]), (lambda: self.theirs[kind].at[slot])
-        yield from reduce_colour(self.me, self.copies, i, kind, c, grads, lambda c, p: self.buffers[kind, (c, p)].at[slot], last)
+        keep = self.kept[c] if i == 0 else None
+        yield from reduce_colour(self.me, self.copies, i, kind, c, grads, lambda c, p: self.buffers[kind, (c, p)].at[slot], last, keep)
 
     def finish(self, i):
         (kind, j), me, copies = ORDER[i], self.me, self.copies
@@ -361,6 +368,7 @@
     for kind in (WIDE, TALL):
         for k in reduce_buffers(kind):
             buffers[kind, k] = rest.pop(0)
+    tall_kept = take(3)
     me = Me()
 
     def fetch(src, dst, sem):
@@ -396,14 +404,20 @@
 
     loads = [fetch(x_in, back, load.at[0]), fetch(dy_in, dy, load.at[1])]
     zeroth = stream(columns(w_gate, 0, tile_g, sem_g), columns(w_up, 0, tile_u, sem_u), n=10)
-    down = stream(columns(w_down, 0, columns_w, sem_c), n=4)
+
+    def half_columns(i, half):
+        src = w_down.at[0, pl.ds(half * 1280, 1280), at_tile(i, 256)]
+        return pltpu.make_async_copy(src, columns_w.at[half], sem_c.at[half])
+
+    for half in (0, 1):
+        half_columns(0, half).start()
     me.barrier()
     own = {WIDE: wide_own, TALL: tall_own}
     theirs = {WIDE: wide_theirs, TALL: tall_theirs}
     halves = {WIDE: lambda: wide_own.at[2], TALL: lambda: tall_half}
     sums = {WIDE: wide_sums, TALL: tall_sums}
     cross = {WIDE: wide_cross, TALL: tall_cross}
-    reduce = Reduce(me, own, theirs, halves, buffers, sums, cross, shares, outs, send, recv, free)
+    reduce = Reduce(me, own, theirs, halves, buffers, sums, cross, shares, outs, send, recv, free, tall_kept)
 
     def ticks(phase, i):
         orders = TICKS[phase]
@@ -477,8 +491,16 @@
 
     @pl.loop(0, 4)
     def _(i):
-        down(i)
-        part = dot(both[0], columns_w[rem(i, 2)]).astype(BF16).astype(F32)
+        part = 0.0
+        for half in (0, 1):
+            half_columns(i, half).wait()
+            part += dot(both[0, :, half * 1280 : half * 1280 + 1280], columns_w[half])
+
+            @pl.when(i < 3)
+            def _():
+                half_columns(i + 1, half).start()
+
+        part = part.astype(BF16).astype(F32)
         back[:, at_tile(i, 256)] = (back[:, at_tile(i, 256)].astype(F32) + part).astype(BF16)
 
     keep.wait()
@@ -583,7 +605,7 @@
     scratch += [pltpu.VMEM((2, 1024, 256), F32)] * 2
     scratch += [pltpu.VMEM((2, 1024, 256), BF16)] * 2 + [pltpu.VMEM((2, 256, 1024), BF16), pltpu.VMEM((2, 256, 2560), BF16)]
     scratch += [
-        pltpu.VMEM((2, 2560, 256), BF16),
+        pltpu.VMEM((2, 1280, 256), BF16),
         pltpu.VMEM((3, *full_shape(WIDE)), BF16),
         pltpu.VMEM((2, *full_shape(WIDE)), BF16),
         pltpu.VMEM((1, *full_shape(TALL)), BF16),
@@ -602,6 +624,7 @@
     ]
     for kind, many in ((WIDE, 2), (TALL, 1)):
         scratch += [pltpu.VMEM((many, *shape), BF16) for shape in reduce_buffers(kind).values()]
+    scratch += [pltpu.VMEM(block(TALL, c, [d for d in "xyz" if d != COLOURS[c][0][0]]), BF16) for c in range(3)]
     kept = [jax.ShapeDtypeStruct((1024, 2560), F32)] * 2 + [jax.ShapeDtypeStruct((1024, 1024), BF16)] * 2
     return pl.pallas_call(
         step_kernel,
@@ -671,15 +694,45 @@
 
 
 def gather_kernel(*refs):
-    wide, tall, outs, rest = refs[0], refs[1], refs[2:8], refs[8:]
-    cross = {WIDE: rest[0], TALL: rest[1]}
-    forty, send, recv = rest[2:5]
+    wide_sums, tall_sums, m, v, weights = refs[0], refs[1], refs[2:5], refs[5:8], refs[8:11]
+    outs, new_m, new_v, rest = refs[11:17], refs[17:20], refs[20:23], refs[23:]
+    wide, tall = rest[:2]
+    cross = {WIDE: rest[2], TALL: rest[3]}
+    rows = {WIDE: rest[4], TALL: rest[5]}
+    forty, load, send, recv = rest[6:10]
     me = Me()
+    mine = 2 * lax.rem(me.at["z"], 2) + me.core
+
+    def which(i):
+        kind, j = ORDER[i]
+        return (2, j) if kind == TALL else (j // 2, j % 2)
+
+    loads = []
+    for i, (kind, j) in enumerate(ORDER):
+        n, layer = which(i)
+        group = me.at["x"] * SIZES["y"] + me.at["y"]
+        z = me.at["z"] if kind == WIDE else lax.div(me.at["z"], 2)
+        first = (group * dims(kind, "z")[0] + z) * ROWS[kind]
+        src = weights[n].at[layer, pl.ds(pl.multiple_of(first, 8), ROWS[kind]), :]
+        loads.append(pltpu.make_async_copy(src, rows[kind].at[j], load.at[i]))
+        loads[-1].start()
     me.barrier()
     copies = Copies(send, recv)
-    mine = 2 * lax.rem(me.at["z"], 2) + me.core
 
     for i, (kind, j) in enumerate(ORDER):
+        n, layer = which(i)
+        loads[i].wait()
+        many, width = (2, HALF[WIDE]) if kind == WIDE else (4, HALF[TALL] // 2)
+        for q in range(many):
+            at = pl.ds((q if kind == WIDE else q % 2 * 2 + q // 2) * width, width)
+            w = rows[kind][j, :, at].astype(F32)
+            size = ROWS[kind] // many
+            own = w[:size]
+            for p in range(1, many):
+                own = jnp.where((me.core if kind == WIDE else mine) == p, w[p * size : (p + 1) * size], own)
+            sums, fresh = (wide_sums, wide) if kind == WIDE else (tall_sums, tall)
+            value, new_m[n][layer, :, at], new_v[n][layer, :, at] = adamw(own, m[n][layer, :, at], v[n][layer, :, at], sums[j, q])
+            fresh[j, q] = value.astype(F32)
         if kind == WIDE:
             copies.start((i, "rows"), lambda j=j: (wide.at[j, 1 - me.core], cross[WIDE].at[j], me.device(core=1 - me.core)))
         else:
@@ -717,32 +770,42 @@
     copies.sent()
 
 
-def all_gather(wide, tall):
+def all_gather(wide, tall, m, v, weights):
+    moments = [pltpu.VMEM(t.shape, F32) for t in m]
     scratch = [
+        pltpu.VMEM((4, 2, 4, 1280), F32),
+        pltpu.VMEM((2, 4, 10, 256), F32),
         pltpu.VMEM((4, 4, 1280), F32),
         pltpu.VMEM((2, 4, 10, 256), F32),
+        pltpu.VMEM((4, ROWS[WIDE], 2560), BF16),
+        pltpu.VMEM((2, ROWS[TALL], 1024), BF16),
         pltpu.VMEM((40, 256), F32),
+        pltpu.SemaphoreType.DMA((6,)),
         pltpu.SemaphoreType.DMA((384,)),
         pltpu.SemaphoreType.DMA((384,)),
     ]
+    matrices = [pltpu.VMEM((*dims(kind, ("x", "y", "z")), ROWS[kind], 2 * HALF[kind]), BF16) for kind, _ in ORDER]
     return pl.pallas_call(
         gather_kernel,
-        out_shape=tuple(pltpu.VMEM((*dims(kind, ("x", "y", "z")), ROWS[kind], 2 * HALF[kind]), BF16) for kind, _ in ORDER),
-        in_specs=[pl.BlockSpec(memory_space=pltpu.VMEM)] * 2,
-        out_specs=(pl.BlockSpec(memory_space=pltpu.VMEM),) * 6,
+        out_shape=(*matrices, *moments, *moments),
+        in_specs=[pl.BlockSpec(memory_space=pltpu.VMEM)] * 8 + [pl.BlockSpec(memory_space=pl.ANY)] * 3,
+        out_specs=(pl.BlockSpec(memory_space=pltpu.VMEM),) * 12,
         scratch_shapes=scratch,
         compiler_params=pltpu.CompilerParams(collective_id=1, has_side_effects=True, vmem_limit_bytes=4 * 1024 * 1024),
         name="all_gather",
-    )(wide, tall)
+    )(wide, tall, *m, *v, *weights)
 
 
 def spill_kernel(*refs):
-    ins, outs, sem = refs[:6], refs[6:9], refs[9]
+    ins, moments, outs, sem = refs[:6], refs[6:12], refs[12:21], refs[21]
     copies = []
     for i, (kind, j) in enumerate(ORDER):
         which, layer = (2, j) if kind == TALL else (j // 2, j % 2)
         copies.append(pltpu.make_async_copy(ins[i], outs[which].at[layer], sem.at[i]))
-        copies[-1].start()
+    for i in range(6):
+        copies.append(pltpu.make_async_copy(moments[i], outs[3 + i], sem.at[6 + i]))
+    for copy in copies:
+        copy.start()
     for copy in copies:
         copy.wait()
 
@@ -751,10 +814,10 @@
     wide, tall = ((2, *dims(kind, ("x", "y", "z")), ROWS[kind], 2 * HALF[kind]) for kind in (WIDE, TALL))
     return pl.pallas_call(
         spill_kernel,
-        out_shape=tuple(jax.ShapeDtypeStruct(shape, BF16) for shape in (wide, wide, tall)),
-        in_specs=[pl.BlockSpec(memory_space=pltpu.VMEM)] * 6,
-        out_specs=(pl.BlockSpec(memory_space=pl.ANY),) * 3,
-        scratch_shapes=[pltpu.SemaphoreType.DMA((6,))],
+        out_shape=(*(jax.ShapeDtypeStruct(shape, BF16) for shape in (wide, wide, tall)), *(jax.ShapeDtypeStruct(t.shape, F32) for t in new[6:])),
+        in_specs=[pl.BlockSpec(memory_space=pltpu.VMEM)] * 12,
+        out_specs=(pl.BlockSpec(memory_space=pl.ANY),) * 9,
+        scratch_shapes=[pltpu.SemaphoreType.DMA((12,))],
         compiler_params=pltpu.CompilerParams(vmem_limit_bytes=1024 * 1024),
         name="spill",
     )(*new)
@@ -767,31 +830,11 @@
     return (w - 0.02 * step).astype(BF16), m, v
 
 
-def rows_of(wide, tall):
-    wide = wide.transpose(0, 2, 1, 3).reshape(2, 2, 4, 2560)
-    tall = tall.reshape(2, 2, 2, 10, 256).transpose(0, 3, 2, 1, 4).reshape(2, 10, 1024)
-    return wide[0], wide[1], tall
-
-
-def gathered(gate, up, down):
-    wide = jnp.stack([gate, up]).reshape(4, 4, 2, 1280).transpose(0, 2, 1, 3).astype(F32)
-    tall = down.reshape(2, 10, 2, 2, 256).transpose(0, 3, 2, 1, 4).reshape(2, 4, 10, 256).astype(F32)
-    new = spill(all_gather(wide, tall))
-    return tuple(w.reshape(2, -1, w.shape[-1]) for w in new)
-
-
 def solution(mesh):
     def step(x, dy, *arrays):
         weights, m, v = (arrays[i : i + 3] for i in (0, 3, 6))
-        gradients = rows_of(*summed(x[0], dy[0], *weights))
-        index = lax.axis_index("dp")
-        news = []
-        for w, mm, vv, g in zip(weights, m, v, gradients, strict=True):
-            rows = mm.shape[1]
-            mine = lax.dynamic_slice_in_dim(w, index * rows, rows, 1)
-            news.append(adamw(mine.astype(F32), mm, vv, g))
-        new = gathered(*(n[0] for n in news))
-        return (*new, *(n[1] for n in news), *(n[2] for n in news))
+        new = spill(all_gather(*summed(x[0], dy[0], *weights), m, v, weights))
+        return (*(w.reshape(2, -1, w.shape[-1]) for w in new[:3]), *new[3:])
 
     batch, whole, rows = P(("rep", "dp")), P(), P(None, "dp")
     return jax.shard_map(

time: 296 us -> 293 us (0.990)
  local copies, waits for them, and re-layouts: 3.69 us -> 15.7 us
  Pallas kernels: 287 us -> 276 us
  other arithmetic: 3.9 us -> 0 us
    unnamed x0 -> x22, local copies, waits for them, and re-layouts: none -> 15.7 us
    pallas_call x1, Pallas kernels: 194 us -> 181 us  [summed(): pl.pallas_call(step_kernel, out_shape=(jax.ShapeDtypeStruct((4, 2, 4, 128...]
where the time goes in v2:
time: 293 us; the launch traced here: 292 us
  Pallas kernels  276 us (94%)
  local copies, waits for them, and re-layouts  15.7 us (5%)
    pallas_call x1, Pallas kernels, summed(): pl.pallas_call(step_kernel, out_shape=(jax.ShapeDtypeStruct((4, 2, 4, 128...  181 us
    pallas_call x1, Pallas kernels, all_gather(): pl.pallas_call(gather_kernel, out_shape=(*matrices, *moments, *moments),...  84.7 us
    unnamed x22, local copies, waits for them, and re-layouts  15.7 us
    pallas_call x1, Pallas kernels, spill(): pl.pallas_call(spill_kernel, out_shape=(*(jax.ShapeDtypeStruct(shape, BF1...  10.5 us

profile of v2, /device:TPU:1, one launch (start us, length us, event | category | flops | bytes accessed | tf_op | source)
XLA Modules:
  0.0 292.1 jit_solution(479165523357874941)
XLA Ops:
  0.6 1.6 copy.20.refs_4_
  2.2 1.6 copy.21.refs_7_
  3.8 180.5 %step.1 = (f32[4,2,4,1280]{3,2,1,0:T(4,128)}, f32[2,4,10,256]{3,2,1,0:T(8,128)}, f32[1024,2560]{1,0:T(8,128)}, f32[1024,2560]{1,0:T(8,128)}, bf16[1024,1024]{1,0:T(8,128)(2,1)}, /*index=5*/bf16[1024,1024]{1,0:T(8,128)(2,1)}) custom-call(bf16[1024,1024]{1,0:T(8,128)(2,1)} %bitcast.5, bf16[1024,1024]{1,0:T(8,128)(2,1)} %bitcast.6, ...), custom_call_target="tpu_custom_call" | custom-call | tf_op jit(solution)/shard_map/step/pallas_call | solution.py:629
  184.3 0.0 copy-start
  184.3 4.0 %copy-done = bf16[2,1024,2560]{2,1,0:T(8,128)(2,1)S(1)} copy-done((bf16[2,1024,2560]{2,1,0:T(8,128)(2,1)S(1)}, bf16[2,1024,2560]{2,1,0:T(8,128)(2,1)}, u32[]{:S(2)}) %copy-start) | copy-done | bytes 10485784
  188.3 0.0 copy-start.1
  188.3 0.9 copy-done.1
  189.2 0.0 copy-start.2
  189.2 0.9 copy-done.2
  190.1 0.0 copy-start.3
  190.1 0.9 copy-done.3
  191.0 0.0 copy-start.4
  191.0 0.9 copy-done.4
  191.9 0.0 copy-start.5
  191.9 0.9 copy-done.5
  192.8 0.0 copy-start.6
  192.8 0.9 copy-done.6
  193.7 0.0 copy-start.7
  193.7 0.9 copy-done.7
  194.6 0.0 copy-start.8
  194.6 0.9 copy-done.8
  195.5 84.7 %all_gather.1 = (bf16[4,4,4,40,1024]{4,3,2,1,0:T(8,128)(2,1)S(1)}, bf16[4,4,8,8,2560]{4,3,2,1,0:T(8,128)(2,1)S(1)}, bf16[4,4,8,8,2560]{4,3,2,1,0:T(8,128)(2,1)S(...) custom-call(f32[4,2,4,1280]{3,2,1,0:T(4,128)S(1)} %copy-done.3, ...), custom_call_target="tpu_custom_call" | custom-call | tf_op jit(solution)/shard_map/all_gather/pallas_call | solution.py:788
  280.2 10.5 %spill.1 = (bf16[2,4,4,8,8,2560]{5,4,3,2,1,0:T(8,128)(2,1)}, bf16[2,4,4,8,8,2560]{5,4,3,2,1,0:T(8,128)(2,1)}, bf16[2,4,4,4,40,1024]{5,4,3,2,1,0:T(8,128)(2,1)}, ...) custom-call(bf16[4,4,4,40,1024]{4,3,2,1,0:T(8,128)(2,1)S(1)} %get-tu, ...), custom_call_target="tpu_custom_call" | custom-call | tf_op jit(solution)/shard_map/spill/pallas_call | solution.py:815
  290.7 0.7 copy.22
  291.4 0.7 copy.23
Async XLA Ops:
  184.3 4.0 %copy-start = (bf16[2,1024,2560]{2,1,0:T(8,128)(2,1)S(1)}, bf16[2,1024,2560]{2,1,0:T(8,128)(2,1)}, u32[]{:S(2)}) copy-start(bf16[2,1024,2560]{2,1,0:T(8,128)(2,1)} %refs_8_.1) | copy-start | bytes 31457284
  188.3 0.9 copy-start.1
  189.2 0.9 copy-start.2
  190.1 0.9 copy-start.3
  191.0 0.9 copy-start.4
  191.9 0.9 copy-start.5
  192.8 0.9 copy-start.6
  193.7 0.9 copy-start.7
  194.6 0.9 copy-start.8

commit v3 on v2

--- a/solution.py
+++ b/solution.py
@@ -15,14 +15,14 @@
 
 TICKS = {
     "first": ["0h"],
-    "wide1": ["1h", "1s020100", "2h121110", "0200"],
-    "back": ["0112222120", "", "02111000", "12", "0122", "022120", "121100", "01102221020s"],
-    "units": ["010012021110222120", "", "0211121021222001", "0003", "122022", "03111013", "132221", "2023", "23", ""],
+    "wide1": ["1h", "1s010200", "2h121011", "0200"],
+    "back": ["0112212022", "", "10020011", "12", "0122", "02002120", "1211", "0110002221020s"],
+    "units": ["011210020020112122", "", "10121121022022", "0103", "1220", "031022", "111321", "13202223", "23", ""],
     "last": ["3h"],
-    "wide0": ["4h", "4s323130", "5h424140", "3230"],
-    "tail": ["42523151504041324230523150325142413040315251323042405041523151403050324142515250324231335240414333514350525353"],
+    "wide0": ["4h", "4s313230", "5h404241", "3230"],
+    "tail": ["31524250514041323052423150513241523040314251303250404152314251504132405230514250313233524142404333435152505353"],
 }
-GATHER_ORDER = "020100121110222120323130424140525150021222324252010011021000122122203210420031520130112120411040300051203150014002301121124150223210014240005251000211122120225031323001414201115211100210214012512122203132422052500241301202302251124022324240313252425031524150415151"
+GATHER_ORDER = "023120220100113012321040412152514250022212325242312002012220001211322030520042103101403011410020102131014051023011504110221200313220522120514201024022301150411231323110520142000111210250510011412240123221305242300210510222501012412232124041322152504240215152504251"
 
 
 RING, DIRECT = "ring", "direct"
@@ -31,11 +31,24 @@
     (("y", RING), ("x", RING), ("z", DIRECT)),
     (("z", RING), ("x", DIRECT), ("y", DIRECT)),
 )
-WIDE, TALL = "wide", "tall"
-PART = {WIDE: ((0, 512), (512, 384), (896, 384)), TALL: ((0, 8), (8, 16), (24, 16))}
-HALF = {WIDE: 1280, TALL: 512}
-ROWS = {WIDE: 8, TALL: 40}
-ORDER = ((TALL, 1), (WIDE, 1), (WIDE, 3), (TALL, 0), (WIDE, 0), (WIDE, 2))
+GATE, UP, TALL = KINDS = "gate", "up", "tall"
+PART = {
+    GATE: ((0, 512), (512, 384), (896, 384)),
+    UP: ((0, 512), (512, 384), (896, 384)),
+    TALL: ((0, 8), (8, 16), (24, 16)),
+}
+GATHER_PART = {
+    GATE: ((0, 512), (512, 384), (896, 384)),
+    UP: ((0, 256), (256, 384), (640, 640)),
+    TALL: ((0, 16), (16, 16), (32, 8)),
+}
+HALF = {GATE: 1280, UP: 1280, TALL: 512}
+ROWS = {GATE: 8, UP: 8, TALL: 40}
+ORDER = ((TALL, 1), (GATE, 1), (UP, 3), (TALL, 0), (GATE, 0), (UP, 2))
+
+
+def by_kind(wide, tall):
+    return {GATE: wide, UP: wide, TALL: tall}
 
 
 class Me:
@@ -59,7 +72,7 @@
         core = self.core if core is None else core
         return (0, ((at["x"] * SIZES["y"] + at["y"]) * SIZES["z"] + at["z"]) * 2 + core)
 
-    def barrier(self):
+    def arrive(self):
         sem = pltpu.get_barrier_semaphore()
 
         def signal(peer):
@@ -69,6 +82,9 @@
             each(n - 1, lambda i, d=d: signal(self.device(**{d: self.off(d, i + 1)})))
         signal(self.device(core=1 - self.core))
         signal(self.device(core=1 - self.core, z=self.pair()))
+        return sem
+
+    def arrived(self, sem):
         pl.semaphore_wait(sem, sum(SIZES.values()) - 1)
 
     def pair(self):
@@ -79,15 +95,15 @@
     return tuple(SIZES[d] // (2 if kind == TALL and d == "z" else 1) for d in free)
 
 
-def view(ref, kind, free, fixed, colour=None, base=0, own=False):
+def view(ref, kind, free, fixed, colour=None, base=0, own=False, parts=PART):
     index = [(fixed[d] // 2 if kind == TALL and d == "z" else fixed[d]) if d in fixed else slice(None) for d in free]
     if own and not (kind == TALL and "z" in free and "z" in fixed):
         return ref.at[(*index, slice(None), slice(None))]
-    if kind == WIDE:
-        first, size = (0, HALF[WIDE]) if colour is None else PART[WIDE][colour]
+    if kind != TALL:
+        first, size = (0, HALF[kind]) if colour is None else parts[kind][colour]
         rows, columns = slice(None), pl.ds(_at(base, first), size)
     else:
-        rows = slice(None) if own or colour is None else pl.ds(*PART[TALL][colour])
+        rows = slice(None) if own or colour is None else pl.ds(*parts[TALL][colour])
         if "z" in free and "z" in fixed:
             columns = pl.ds(pl.multiple_of(base + lax.rem(fixed["z"], 2) * 256, 256), 256)
         else:
@@ -101,7 +117,7 @@
 
 def block(kind, colour, free):
     first, size = PART[kind][colour]
-    tail = (8, size) if kind == WIDE else (size, HALF[TALL] if "z" in free else HALF[TALL] // 2)
+    tail = (8, size) if kind != TALL else (size, HALF[TALL] if "z" in free else HALF[TALL] // 2)
     return dims(kind, free) + tail
 
 
@@ -273,22 +289,22 @@
 
         def last(colour, value):
             first, size = PART[kind][colour]
-            if kind == WIDE:
-                self.sums[WIDE][j, 0, :, first : first + size] = value[:4]
-                self.sums[WIDE][j, 1, :, first : first + size] = value[4:]
+            if kind != TALL:
+                self.sums[kind][j, 0, :, first : first + size] = value[:4]
+                self.sums[kind][j, 1, :, first : first + size] = value[4:]
             else:
                 self.sums[TALL][j, first : first + size, :] = value
 
         grads = (lambda: self.own[kind].at[slot]), (lambda: self.theirs[kind].at[slot])
         keep = self.kept[c] if i == 0 else None
-        yield from reduce_colour(self.me, self.copies, i, kind, c, grads, lambda c, p: self.buffers[kind, (c, p)].at[slot], last, keep)
+        yield from reduce_colour(self.me, self.copies, i, kind, c, grads, lambda c, p: self.buffers[kind, (c, p)].at[0], last, keep)
 
     def finish(self, i):
         (kind, j), me, copies = ORDER[i], self.me, self.copies
         sums, cross, shares, outs = self.sums, self.cross, self.shares, self.outs
         mine = 2 * lax.rem(me.at["z"], 2) + me.core
-        if kind == WIDE:
-            copies.start((i, "rows"), lambda: (sums[WIDE].at[j, 1 - me.core], cross[WIDE].at[j], me.device(core=1 - me.core)))
+        if kind != TALL:
+            copies.start((i, "rows"), lambda: (sums[kind].at[j, 1 - me.core], cross[kind].at[j], me.device(core=1 - me.core)))
         else:
             for q in range(4):
                 shares[j, q] = sums[TALL][j, 10 * q : 10 * q + 10, :]
@@ -306,10 +322,10 @@
             self.done(i, me.device(core=1 - me.core))
         yield
         mine = 2 * lax.rem(me.at["z"], 2) + me.core
-        if kind == WIDE:
+        if kind != TALL:
             copies.arrived((i, "rows"))
-            outs[0][j, me.core] = sums[WIDE][j, me.core]
-            outs[0][j, 1 - me.core] = cross[WIDE][j]
+            outs[0][j, me.core] = sums[kind][j, me.core]
+            outs[0][j, 1 - me.core] = cross[kind][j]
         else:
             for o in range(3):
                 copies.arrived((i, "rows", o))
@@ -365,7 +381,7 @@
     wide_sums, tall_sums, wide_cross, tall_cross, shares = take(5)
     load, sem_g, sem_u, sem_d, sem_w, sem_c, sem_f, send, recv, free = take(10)
     buffers = {}
-    for kind in (WIDE, TALL):
+    for kind in KINDS:
         for k in reduce_buffers(kind):
             buffers[kind, k] = rest.pop(0)
     tall_kept = take(3)
@@ -411,12 +427,11 @@
 
     for half in (0, 1):
         half_columns(0, half).start()
-    me.barrier()
-    own = {WIDE: wide_own, TALL: tall_own}
-    theirs = {WIDE: wide_theirs, TALL: tall_theirs}
-    halves = {WIDE: lambda: wide_own.at[2], TALL: lambda: tall_half}
-    sums = {WIDE: wide_sums, TALL: tall_sums}
-    cross = {WIDE: wide_cross, TALL: tall_cross}
+    peers = me.arrive()
+    own = by_kind(wide_own, tall_own)
+    theirs = by_kind(wide_theirs, tall_theirs)
+    halves = by_kind(lambda: wide_own.at[2], lambda: tall_half)
+    sums, cross = by_kind(wide_sums, tall_sums), by_kind(wide_cross, tall_cross)
     reduce = Reduce(me, own, theirs, halves, buffers, sums, cross, shares, outs, send, recv, free, tall_kept)
 
     def ticks(phase, i):
@@ -431,10 +446,9 @@
             h = back[rows, :].astype(F32)
             act[rows, :] = (h * lax.rsqrt(jnp.mean(h * h, -1, keepdims=True) + 1e-6)).astype(BF16)
 
-    def turn(src):
-        @pl.loop(0, 8)
-        def _(i):
-            turned[:, at_tile(i, 128)] = src[at_tile(i, 128), :].T
+    def turn(src, i):
+        i = rem(i, 8)
+        turned[:, at_tile(i, 128)] = src[at_tile(i, 128), :].T
 
     def unit(i, g, u, d, dout):
         d = d.astype(BF16).astype(F32)
@@ -460,8 +474,7 @@
         pairs = (gates.at[slot], gate_kept.at[:, at_tile(i, 256)]), (ups.at[slot], up_kept.at[:, at_tile(i, 256)])
         return [pltpu.make_async_copy(*(p if out else p[::-1]), sem_f.at[n, slot]) for n, p in enumerate(pairs)]
 
-    for copy in loads:
-        copy.wait()
+    loads[0].wait()
     norm()
     keep = fetch(act, a0_kept, load.at[0])
 
@@ -506,14 +519,17 @@
     keep.wait()
     keep = fetch(back, h1_kept, load.at[0])
     norm()
-    turn(act)
+
+    loads[1].wait()
 
     @pl.loop(0, 10)
     def _(i):
         first(i)
+        turn(act, i)
         slot = rem(i, 2)
         unit(i, dot(act[...], tile_g[slot]), dot(act[...], tile_u[slot]), dot(dy[...], tile_d[slot], 1, 1), dy)
 
+    me.arrived(peers)
     reduce.run(TICKS["first"][0])
     wide_grads("wide1")
 
@@ -564,7 +580,6 @@
     for copy in kept(0, False):
         copy.start()
     load_a.wait()
-    turn(back)
 
     @pl.loop(0, 10)
     def _(i):
@@ -574,6 +589,7 @@
                 copy.start()
 
         second(i)
+        turn(back, i)
         for copy in kept(i, False):
             copy.wait()
         slot = rem(i, 2)
@@ -606,8 +622,8 @@
     scratch += [pltpu.VMEM((2, 1024, 256), BF16)] * 2 + [pltpu.VMEM((2, 256, 1024), BF16), pltpu.VMEM((2, 256, 2560), BF16)]
     scratch += [
         pltpu.VMEM((2, 1280, 256), BF16),
-        pltpu.VMEM((3, *full_shape(WIDE)), BF16),
-        pltpu.VMEM((2, *full_shape(WIDE)), BF16),
+        pltpu.VMEM((3, *full_shape(GATE)), BF16),
+        pltpu.VMEM((2, *full_shape(GATE)), BF16),
         pltpu.VMEM((1, *full_shape(TALL)), BF16),
         pltpu.VMEM(full_shape(TALL), BF16),
         pltpu.VMEM((1, *full_shape(TALL)), BF16),
@@ -622,8 +638,8 @@
         pltpu.SemaphoreType.DMA((256,)),
         pltpu.SemaphoreType.REGULAR((3,)),
     ]
-    for kind, many in ((WIDE, 2), (TALL, 1)):
-        scratch += [pltpu.VMEM((many, *shape), BF16) for shape in reduce_buffers(kind).values()]
+    for kind in KINDS:
+        scratch += [pltpu.VMEM((1, *shape), BF16) for shape in reduce_buffers(kind).values()]
     scratch += [pltpu.VMEM(block(TALL, c, [d for d in "xyz" if d != COLOURS[c][0][0]]), BF16) for c in range(3)]
     kept = [jax.ShapeDtypeStruct((1024, 2560), F32)] * 2 + [jax.ShapeDtypeStruct((1024, 1024), BF16)] * 2
     return pl.pallas_call(
@@ -642,7 +658,7 @@
     fixed = dict(me.at)
 
     def part(at):
-        return view(ref, kind, ("x", "y", "z"), at, colour, base)
+        return view(ref, kind, ("x", "y", "z"), at, colour, base, parts=GATHER_PART)
 
     phases = COLOURS[colour][::-1]
     for phase, (d, how) in enumerate(phases):
@@ -694,11 +710,12 @@
 
 
 def gather_kernel(*refs):
-    wide_sums, tall_sums, m, v, weights = refs[0], refs[1], refs[2:5], refs[5:8], refs[8:11]
+    given, weights = refs[:8], refs[8:11]
     outs, new_m, new_v, rest = refs[11:17], refs[17:20], refs[20:23], refs[23:]
+    taken, rest = rest[:8], rest[8:]
+    wide_sums, tall_sums, m, v = taken[0], taken[1], taken[2:5], taken[5:8]
     wide, tall = rest[:2]
-    cross = {WIDE: rest[2], TALL: rest[3]}
-    rows = {WIDE: rest[4], TALL: rest[5]}
+    cross, rows = by_kind(*rest[2:4]), by_kind(*rest[4:6])
     forty, load, send, recv = rest[6:10]
     me = Me()
     mine = 2 * lax.rem(me.at["z"], 2) + me.core
@@ -708,47 +725,56 @@
         return (2, j) if kind == TALL else (j // 2, j % 2)
 
     loads = []
+    takes = [pltpu.make_async_copy(*pair, load.at[6 + n]) for n, pair in enumerate(zip(given, taken, strict=True))]
+    for copy in takes:
+        copy.start()
     for i, (kind, j) in enumerate(ORDER):
         n, layer = which(i)
         group = me.at["x"] * SIZES["y"] + me.at["y"]
-        z = me.at["z"] if kind == WIDE else lax.div(me.at["z"], 2)
+        z = me.at["z"] if kind != TALL else lax.div(me.at["z"], 2)
         first = (group * dims(kind, "z")[0] + z) * ROWS[kind]
         src = weights[n].at[layer, pl.ds(pl.multiple_of(first, 8), ROWS[kind]), :]
         loads.append(pltpu.make_async_copy(src, rows[kind].at[j], load.at[i]))
         loads[-1].start()
-    me.barrier()
+    peers = me.arrive()
     copies = Copies(send, recv)
-
-    for i, (kind, j) in enumerate(ORDER):
+    for copy in takes:
+        copy.wait()
+
+    def update(i):
+        kind, j = ORDER[i]
         n, layer = which(i)
         loads[i].wait()
-        many, width = (2, HALF[WIDE]) if kind == WIDE else (4, HALF[TALL] // 2)
+        many, width = (2, HALF[kind]) if kind != TALL else (4, HALF[TALL] // 2)
         for q in range(many):
-            at = pl.ds((q if kind == WIDE else q % 2 * 2 + q // 2) * width, width)
+            at = pl.ds((q if kind != TALL else q % 2 * 2 + q // 2) * width, width)
+            here = (layer, slice(None), at) if kind != TALL else (slice(None), layer, at)
             w = rows[kind][j, :, at].astype(F32)
             size = ROWS[kind] // many
             own = w[:size]
             for p in range(1, many):
-                own = jnp.where((me.core if kind == WIDE else mine) == p, w[p * size : (p + 1) * size], own)
-            sums, fresh = (wide_sums, wide) if kind == WIDE else (tall_sums, tall)
-            value, new_m[n][layer, :, at], new_v[n][layer, :, at] = adamw(own, m[n][layer, :, at], v[n][layer, :, at], sums[j, q])
+                own = jnp.where((me.core if kind != TALL else mine) == p, w[p * size : (p + 1) * size], own)
+            sums, fresh = (wide_sums, wide) if kind != TALL else (tall_sums, tall)
+            value, new_m[n][here], new_v[n][here] = adamw(own, m[n][here], v[n][here], sums[j, q])
             fresh[j, q] = value.astype(F32)
-        if kind == WIDE:
-            copies.start((i, "rows"), lambda j=j: (wide.at[j, 1 - me.core], cross[WIDE].at[j], me.device(core=1 - me.core)))
+        if not copies.used:
+            me.arrived(peers)
+        if kind != TALL:
+            copies.start((i, "rows"), lambda: (wide.at[j, 1 - me.core], cross[kind].at[j], me.device(core=1 - me.core)))
         else:
             for o, (z, core) in enumerate(((me.at["z"], 1 - me.core), (me.pair(), me.core), (me.pair(), 1 - me.core))):
                 q = 2 * lax.rem(z, 2) + core
                 copies.start(
                     (i, "rows", o),
-                    lambda j=j, q=q, z=z, core=core: (tall.at[j, q], cross[TALL].at[j, mine], me.device(core=core, z=z)),
+                    lambda q=q, z=z, core=core: (tall.at[j, q], cross[TALL].at[j, mine], me.device(core=core, z=z)),
                 )
 
     def begin(i):
         kind, j = ORDER[i]
         here = view(outs[i], kind, ("x", "y", "z"), me.at, None, me.core * HALF[kind])
-        if kind == WIDE:
+        if kind != TALL:
             copies.arrived((i, "rows"))
-            own, theirs = wide[j, me.core], cross[WIDE][j]
+            own, theirs = wide[j, me.core], cross[kind][j]
             first = me.core == 0
             rows = [jnp.where(first, own, theirs), jnp.where(first, theirs, own)]
             here[...] = jnp.concatenate(rows, axis=0).astype(BF16)
@@ -762,10 +788,15 @@
     def colour(i, c):
         if i in waiting:
             waiting.discard(i)
+            for following in turns[turns.index(i) + 2 :][:1]:
+                update(following)
             begin(i)
         yield from gather_colour(me, copies, i, ORDER[i][0], c, outs[i])
 
     waiting = set(range(6))
+    turns = list(dict.fromkeys(int(i) for i in GATHER_ORDER[::2]))
+    update(turns[0])
+    update(turns[1])
     run({(i, c): colour(i, c) for i in range(6) for c in range(3)}, GATHER_ORDER)
     copies.sent()
 
@@ -773,14 +804,15 @@
 def all_gather(wide, tall, m, v, weights):
     moments = [pltpu.VMEM(t.shape, F32) for t in m]
     scratch = [
+        *(pltpu.VMEM(t.shape, F32) for t in (wide, tall, *m, *v)),
         pltpu.VMEM((4, 2, 4, 1280), F32),
         pltpu.VMEM((2, 4, 10, 256), F32),
         pltpu.VMEM((4, 4, 1280), F32),
         pltpu.VMEM((2, 4, 10, 256), F32),
-        pltpu.VMEM((4, ROWS[WIDE], 2560), BF16),
+        pltpu.VMEM((4, ROWS[GATE], 2560), BF16),
         pltpu.VMEM((2, ROWS[TALL], 1024), BF16),
         pltpu.VMEM((40, 256), F32),
-        pltpu.SemaphoreType.DMA((6,)),
+        pltpu.SemaphoreType.DMA((14,)),
         pltpu.SemaphoreType.DMA((384,)),
         pltpu.SemaphoreType.DMA((384,)),
     ]
@@ -788,10 +820,10 @@
     return pl.pallas_call(
         gather_kernel,
         out_shape=(*matrices, *moments, *moments),
-        in_specs=[pl.BlockSpec(memory_space=pltpu.VMEM)] * 8 + [pl.BlockSpec(memory_space=pl.ANY)] * 3,
+        in_specs=[pl.BlockSpec(memory_space=pl.ANY)] * 11,
         out_specs=(pl.BlockSpec(memory_space=pltpu.VMEM),) * 12,
         scratch_shapes=scratch,
-        compiler_params=pltpu.CompilerParams(collective_id=1, has_side_effects=True, vmem_limit_bytes=4 * 1024 * 1024),
+        compiler_params=pltpu.CompilerParams(collective_id=1, has_side_effects=True, vmem_limit_bytes=28 * 1024 * 1024),
         name="all_gather",
     )(wide, tall, *m, *v, *weights)
 
@@ -811,7 +843,7 @@
 
 
 def spill(new):
-    wide, tall = ((2, *dims(kind, ("x", "y", "z")), ROWS[kind], 2 * HALF[kind]) for kind in (WIDE, TALL))
+    wide, tall = ((2, *dims(kind, ("x", "y", "z")), ROWS[kind], 2 * HALF[kind]) for kind in (GATE, TALL))
     return pl.pallas_call(
         spill_kernel,
         out_shape=(*(jax.ShapeDtypeStruct(shape, BF16) for shape in (wide, wide, tall)), *(jax.ShapeDtypeStruct(t.shape, F32) for t in new[6:])),
@@ -833,8 +865,10 @@
 def solution(mesh):
     def step(x, dy, *arrays):
         weights, m, v = (arrays[i : i + 3] for i in (0, 3, 6))
+        m, v = ((*t[:2], t[2].transpose(1, 0, 2)) for t in (m, v))
         new = spill(all_gather(*summed(x[0], dy[0], *weights), m, v, weights))
-        return (*(w.reshape(2, -1, w.shape[-1]) for w in new[:3]), *new[3:])
+        m, v = ((*t[:2], t[2].transpose(1, 0, 2)) for t in (new[3:6], new[6:9]))
+        return (*(w.reshape(2, -1, w.shape[-1]) for w in new[:3]), *m, *v)
 
     batch, whole, rows = P(("rep", "dp")), P(), P(None, "dp")
     return jax.shard_map(

time: 293 us -> 272 us (0.928)
  local copies, waits for them, and re-layouts: 15.7 us -> 0 us
  Pallas kernels: 276 us -> 271 us
    unnamed x22 -> x0, local copies, waits for them, and re-layouts: 15.7 us -> none
    pallas_call x1, Pallas kernels: 181 us -> 177 us  [summed(): pl.pallas_call(step_kernel, out_shape=(jax.ShapeDtypeStruct((4, 2, 4, 128...]
where the time goes in v3:
time: 272 us; the launch traced here: 271 us
  Pallas kernels  271 us (100%)
    pallas_call x1, Pallas kernels, summed(): pl.pallas_call(step_kernel, out_shape=(jax.ShapeDtypeStruct((4, 2, 4, 128...  177 us
    pallas_call x1, Pallas kernels, all_gather(): pl.pallas_call(gather_kernel, out_shape=(*matrices, *moments, *moments),...  82.9 us
    pallas_call x1, Pallas kernels, spill(): pl.pallas_call(spill_kernel, out_shape=(*(jax.ShapeDtypeStruct(shape, BF1...  10.5 us

profile of v3, /device:TPU:1, one launch (start us, length us, event | category | flops | bytes accessed | tf_op | source)
XLA Modules:
  0.0 271.5 jit_solution(15442353775757363467)
XLA Ops:
  0.6 177.2 %step.1 = (f32[4,2,4,1280]{3,2,1,0:T(4,128)}, f32[2,4,10,256]{3,2,1,0:T(8,128)}, f32[1024,2560]{1,0:T(8,128)}, f32[1024,2560]{1,0:T(8,128)}, bf16[1024,1024]{1,0:T(8,128)(2,1)}, /*index=5*/bf16[1024,1024]{1,0:T(8,128)(2,1)}) custom-call(bf16[1024,1024]{1,0:T(8,128)(2,1)} %bitcast.9, bf16[1024,1024]{1,0:T(8,128)(2,1)} %bitcast.10, ...), custom_call_target="tpu_custom_call" | custom-call | tf_op jit(solution)/shard_map/step/pallas_call | solution.py:645
  177.9 82.9 %all_gather.1 = (bf16[4,4,4,40,1024]{4,3,2,1,0:T(8,128)(2,1)S(1)}, bf16[4,4,8,8,2560]{4,3,2,1,0:T(8,128)(2,1)S(1)}, bf16[4,4,8,8,2560]{4,3,2,1,0:T(8,128)(2,1)S(...) custom-call(f32[4,2,4,1280]{3,2,1,0:T(4,128)} %get-tuple-element.32., ...), custom_call_target="tpu_custom_call" | custom-call | tf_op jit(solution)/shard_map/all_gather/pallas_call | solution.py:820
  260.8 10.5 %spill.1 = (bf16[2,4,4,8,8,2560]{5,4,3,2,1,0:T(8,128)(2,1)}, bf16[2,4,4,8,8,2560]{5,4,3,2,1,0:T(8,128)(2,1)}, bf16[2,4,4,4,40,1024]{5,4,3,2,1,0:T(8,128)(2,1)}, ...) custom-call(bf16[4,4,4,40,1024]{4,3,2,1,0:T(8,128)(2,1)S(1)} %get-tu, ...), custom_call_target="tpu_custom_call" | custom-call | tf_op jit(solution)/shard_map/spill/pallas_call | solution.py:847
